TPU v7x, 256 devices: a whole 4x4x8 slice. The times are simulated.
256 devices in a mesh: dp: 8 (over z_lo, core), expert: 32 (over y, x, z_hi).
Axes of the slice: x: 4, y: 4, z: 8 (z_hi: 2, z_lo: 4; z = z_hi * 4 + z_lo), core: 2. Of those that a mesh axis runs over, the one named last changes fastest.
Arguments:
- tokens: bfloat16 [32768, 3584], P(('dp', 'expert')), may hold values from -6 to 6
- cotangent: bfloat16 [32768, 3584], P(('dp', 'expert')), may hold values from -6 to 6
- gates: float32 [32768, 1], P(('dp', 'expert')), may hold values from 0.1 to 1
- routes: int32 [32768, 1], P(('dp', 'expert')), may hold values from 0 to 31; in each aligned block of 128 rows (0 to 127, 128 to 255, ...) at most 5 rows name the same one
- w_up: bfloat16 [32, 3584, 1024], P('expert', None, 'dp'), may hold values from -0.09375 to 0.09375
- w_down: bfloat16 [32, 1024, 3584], P('expert', 'dp'), may hold values from -0.1875 to 0.1875
- m_up: bfloat16 [32, 3584, 1024], P('expert', None, 'dp'), may hold values from -3 to 3
- v_up: bfloat16 [32, 3584, 1024], P('expert', None, 'dp'), may hold values from 0.099609375 to 1
- m_down: bfloat16 [32, 1024, 3584], P('expert', 'dp'), may hold values from -3 to 3
- v_down: bfloat16 [32, 1024, 3584], P('expert', 'dp'), may hold values from 0.099609375 to 1
- leaving: int32 [1], replicated, may hold values from 0 to 31
- tile_owner: int32 [32], replicated, may hold values from 0 to 31, each once
Outputs:
- update_up: bfloat16 [32, 3584, 1024], P('expert', None, 'dp')
- update_down: bfloat16 [32, 1024, 3584], P('expert', 'dp')
- adopted_up: bfloat16 [32, 112, 1024], P('expert', None, 'dp')
- adopted_down: bfloat16 [32, 112, 1024], P('expert', None, 'dp')
Inputs may be any that keep to these rules, and one draw needn't show every extreme that they name: `routes`: each row names one expert; within the 128 rows of one device no expert is named more than 5 times, a bound that some block reaches in some devices. `tile_owner`: A permutation of the 32 device indices of the expert axis.
All inputs are finite; a program needn't handle non-finite values.
Results may differ from a plain program's by a relative error of at most 0.0041.
Values may be sent and summed in bfloat16 or wider, within the bound.
A program may use at most 128 MiB of HBM per device.

v0:
```python
import jax
import jax.numpy as jnp
from jax import lax
from jax.sharding import PartitionSpec as P

BETA_ONE = 0.9
BETA_TWO = 0.95
EPSILON = 1e-08


def expert_terms(rows_x, rows_c, up_tile, down_tile):
    preact = jnp.dot(rows_x, up_tile, preferred_element_type=jnp.float32)
    squash = jax.nn.sigmoid(preact)
    hidden = (preact * squash).astype(jnp.bfloat16)
    slope_val = squash * (1.0 + preact * (1.0 - squash))
    back_grad = lax.dot_general(
        rows_c, down_tile, (((1,), (1,)), ((), ())), preferred_element_type=jnp.float32
    )
    pre_grad = (back_grad * slope_val).astype(jnp.bfloat16)
    grad_up = lax.dot_general(
        rows_x, pre_grad, (((0,), (0,)), ((), ())), preferred_element_type=jnp.float32
    )
    grad_cols = lax.dot_general(
        rows_c, hidden, (((0,), (0,)), ((), ())), preferred_element_type=jnp.float32
    )
    return (grad_up, grad_cols)


def adam_step(gradient, moment_one, moment_two):
    new_one = BETA_ONE * moment_one.astype(jnp.float32) + (1.0 - BETA_ONE) * gradient
    new_two = BETA_TWO * moment_two.astype(jnp.float32) + (1.0 - BETA_TWO) * gradient * gradient
    return (new_one / (jnp.sqrt(new_two) + EPSILON)).astype(jnp.bfloat16)


def on_device(
    tokens, cotangent, gates, routes, w_up, w_down, m_up, v_up, m_down, v_down, leaving, tile_owner
):
    experts = lax.axis_size("expert")
    my_index = lax.axis_index("expert")
    tok_count, model_width = tokens.shape
    top_count = routes.shape[1]
    hidden_units = w_up.shape[2]
    capacity = 5 * tok_count * top_count // (4 * experts)
    pair_count = tok_count * top_count
    leaver = leaving[0]
    slot_ids = jnp.arange(experts, dtype=jnp.int32)
    tile_rows = model_width // experts
    adopt = jnp.sum(
        jnp.where(tile_owner[None, :] == slot_ids[:, None], slot_ids[None, :], 0), axis=1
    )
    expert_of = routes.reshape(pair_count)
    member = (expert_of[:, None] == slot_ids[None, :]).astype(jnp.int32)
    slot_rank = jnp.sum((jnp.cumsum(member, axis=0) - 1) * member, axis=1)
    slot_place = expert_of * capacity + slot_rank
    staying = expert_of != leaver
    send_mask = jnp.ones_like(staying)
    pair_x = jnp.repeat(tokens, top_count, axis=0)
    pair_c = (
        gates.reshape(pair_count)[:, None]
        * jnp.repeat(cotangent, top_count, axis=0).astype(jnp.float32)
    ).astype(jnp.bfloat16)
    pair_both = jnp.concatenate([pair_x, pair_c], axis=1)
    targets = jnp.arange(experts * capacity, dtype=jnp.int32)
    picker = ((slot_place[None, :] == targets[:, None]) & send_mask[None, :]).astype(jnp.bfloat16)
    send_both = jnp.dot(picker, pair_both, preferred_element_type=jnp.float32).astype(jnp.bfloat16)
    send_x = send_both[:, :model_width].reshape(experts, capacity, model_width)
    send_c = send_both[:, model_width:].reshape(experts, capacity, model_width)
    recv_x, recv_c = (
        lax.all_to_all(send_x, "expert", split_axis=0, concat_axis=0, tiled=True),
        lax.all_to_all(send_c, "expert", split_axis=0, concat_axis=0, tiled=True),
    )
    recv_x = recv_x.reshape(experts * capacity, model_width)
    recv_c = recv_c.reshape(experts * capacity, model_width)
    grad_up, grad_cols = expert_terms(
        lax.all_gather(recv_x, "dp", axis=0, tiled=True),
        lax.all_gather(recv_c, "dp", axis=0, tiled=True),
        w_up[0],
        w_down[0],
    )
    keep_own = my_index != leaver
    step_up = adam_step(grad_up, m_up[0], v_up[0])
    step_down = adam_step(grad_cols.T, m_down[0], v_down[0])
    both_steps = jnp.concatenate([step_up, step_down.T], axis=1).reshape(
        experts, tile_rows, 2 * hidden_units
    )
    ordered = both_steps[adopt]
    outgoing = jnp.where(keep_own, jnp.zeros_like(ordered), ordered)
    incoming = lax.all_to_all(outgoing, "expert", split_axis=0, concat_axis=0, tiled=True)
    mine = lax.dynamic_index_in_dim(incoming, leaver, 0, keepdims=False)
    adopted_up = mine[:, :hidden_units][None]
    adopted_down = mine[:, hidden_units:][None]
    update_up = jnp.where(keep_own, step_up, jnp.zeros_like(step_up))[None]
    update_down = jnp.where(keep_own, step_down, jnp.zeros_like(step_down))[None]
    return (update_up, update_down, adopted_up, adopted_down)


def solution(mesh):
    placed = (
        P(("dp", "expert"), None),
        P(("dp", "expert"), None),
        P(("dp", "expert"), None),
        P(("dp", "expert"), None),
        P("expert", None, "dp"),
        P("expert", "dp", None),
        P("expert", None, "dp"),
        P("expert", None, "dp"),
        P("expert", "dp", None),
        P("expert", "dp", None),
        P(),
        P(),
    )
    return jax.shard_map(
        on_device,
        mesh=mesh,
        in_specs=placed,
        out_specs=(
            P("expert", None, "dp"),
            P("expert", "dp", None),
            P("expert", None, "dp"),
            P("expert", None, "dp"),
        ),
        check_vma=False,
    )
```

profile of v0, /device:TPU:24, one launch (start us, length us, event | category | flops | bytes accessed | tf_op | source)
XLA Modules:
  0.0 399.8 jit_solution(538637933655754063)
XLA Ops:
  7.2 0.0 copy-start
  7.2 0.0 copy-start.7
  7.2 0.0 all-gather.3.cloned.1.call-start
  7.2 0.9 fusion.19
  8.1 0.2 reduce_window_sum.11
  8.3 0.8 select_reduce_fusion
  9.1 0.7 multiply_add_fusion
  9.8 1.4 multiply_convert_fusion
  11.2 0.0 copy-done.7
  11.2 0.7 convolution_convert_fusion
  11.9 1.5 fusion.25
  13.5 1.5 reshape.61
  15.0 61.0 %all_to_all.15 = bf16[32,5,3584]{2,1,0:T(8,128)(2,1)} all-to-all(bf16[32,5,3584]{2,1,0:T(8,128)(2,1)S(1)} %reshape.61), channel_id=1, replica_groups=mesh['dp'=8,'expert'=32] {'expert'}, dimensions={0} | all-to-all | bytes 2293760 | tf_op jit(solution)/shard_map/all_to_all | solution.py:69
  76.0 2.5 reshape.62
  78.5 0.0 all-gather.3.cloned.1.call-update
  78.5 0.0 all-gather.5.cloned.1.call-start
  78.6 1.5 reshape.63
  80.1 62.8 %all_to_all.16 = bf16[32,5,3584]{2,1,0:T(8,128)(2,1)} all-to-all(bf16[32,5,3584]{2,1,0:T(8,128)(2,1)S(1)} %reshape.63), channel_id=1, replica_groups=mesh['dp'=8,'expert'=32] {'expert'}, dimensions={0} | all-to-all | bytes 2293760 | tf_op jit(solution)/shard_map/all_to_all | solution.py:70
  143.0 0.0 copy-start.2
  143.0 2.6 reshape.64
  145.6 0.0 copy-start.3
  145.6 0.0 all-gather.5.cloned.1.call-update
  146.4 0.0 copy-done.2
  146.4 0.0 copy-start.9
  146.4 1.3 copy.24
  147.7 0.0 copy-done.3
  147.7 0.0 copy-start.8
  147.7 1.3 copy.25
  148.9 0.0 copy-done.9
  148.9 0.1 select_reduce_fusion.1
  149.1 52.4 %all-gather.3.cloned.1.call-done = bf16[1280,3584]{1,0:T(8,128)(2,1)} async-done(((bf16[160,3584]{1,0:T(8,128)(2,1)}), bf16[1280,3584]{1,0:T(8,128)(2,1)}) %all-gather.3.cloned.1.call-update) | async-done | bytes 9175056 | tf_op jit(solution)/shard_map/all_gather | solution.py:75
  201.5 0.0 copy-done.8
  201.5 6.2 %fusion.14 = f32[1280,128]{1,0:T(8,128)S(1)} fusion(bf16[1280,3584]{1,0:T(8,128)(2,1)} %all-gather.3.cloned.1.call-done, bf16[1,3584,128]{2,1,0:T(8,128)(2,1)S(1)} %copy-done.8), kind=kOutput, calls=%fused_computation.24 | convolution fusion | flops 1174405120 | bytes 10747904 | tf_op jit(solution)/shard_map/dot_general | solution.py:12
  207.6 0.0 copy-start.5
  207.7 0.0 copy-start.6
  207.7 97.8 %all-gather.5.cloned.1.call-done = bf16[1280,3584]{1,0:T(8,128)(2,1)} async-done(((bf16[160,3584]{1,0:T(8,128)(2,1)}), bf16[1280,3584]{1,0:T(8,128)(2,1)}) %all-gather.5.cloned.1.call-update) | async-done | bytes 9175056 | tf_op jit(solution)/shard_map/all_gather | solution.py:76
  305.4 7.4 %fusion.12 = bf16[128,3584]{1,0:T(8,128)(2,1)} fusion(bf16[1,128,3584]{2,1,0:T(8,128)(2,1)} %param.21, bf16[1,128,3584]{2,1,0:T(8,128)(2,1)} %param.20, bf16[1280,3584]{1,0:T(8,128)(2,1)} %all-gather.5.cloned.1.call-done, f32[1280,128]{1,0:T(8,128)S(1)} %fusion.14), kind=kOutput, calls=%fused_computation.21 | convolution fusion | flops 1180729344 | bytes 12582912 | tf_op jit(solution)/shard_map/dot_general | solution.py:23
  312.9 0.0 copy-done
  312.9 0.0 copy-done.5
  312.9 0.0 copy-done.6
  312.9 14.3 %select_bitcast_fusion.1 = (bf16[1,3584,128]{1,2,0:T(8,128)(2,1)}, bf16[3584,128]{0,1:T(8,128)(2,1)}) fusion(pred[]{:T(512)S(6)} %ne.3, bf16[1,3584,128]{1,2,0:T(8,128)(2,1)S(1)} %copy-done.6, bf16[1,3584,128]{1,2,0:T(8,128)(2,1)S(1)} %copy-done.5, bf16[1280,3584]{1,0:T(8,128)(2,1)} %all-gather.3.cloned.1.call-done, ...), kind=kOutput, calls=%fused_computation.28 | convolution fusion | flops 2356248576 | bytes 23592960 | tf_op jit(solution)/shard_map/dot_general | solution.py:20
  327.2 1.6 pad_maximum_fusion
  328.8 2.3 copy.26
  331.0 2.2 gather_fusion
  333.2 1.4 broadcast_select_fusion
  334.6 0.0 copy-start.4
  334.6 10.1 %all-to-all-start.2 = ((bf16[32,112,256]{2,1,0:T(8,128)(2,1)}), bf16[32,112,256]{2,1,0:T(8,128)(2,1)}, u32[]{:S(2)}, u32[]{:S(2)}) async-start(bf16[32,112,256]{2,1,0:T(8,128)(2,1)} %broadcast_select_fusion), calls=%async_computation.2 | async-start | bytes 3670016 | tf_op jit(solution)/shard_map/all_to_all | solution.py:88
  344.6 0.0 copy-start.1
  344.6 0.0 copy-done.4
  344.7 1.3 copy.27
  345.9 0.0 copy-done.1
  345.9 1.0 select_bitcast_fusion
  346.9 44.6 %all-to-all-done.2 = bf16[32,112,256]{2,1,0:T(8,128)(2,1)} async-done(((bf16[32,112,256]{2,1,0:T(8,128)(2,1)}), bf16[32,112,256]{2,1,0:T(8,128)(2,1)}, u32[]{:S(2)}, u32[]{:S(2)}) %all-to-all-start.2) | async-done | bytes 1835040 | tf_op jit(solution)/shard_map/all_to_all | solution.py:88
  391.6 0.8 dynamic-slice_bitcast_fusion
  392.4 0.6 slice_bitcast_fusion
  (2 shorter events, 0.0 us)
Async XLA Ops:
  7.2 305.7 %copy-start = (bf16[1,128,3584]{2,1,0:T(8,128)(2,1)S(1)}, bf16[1,128,3584]{2,1,0:T(8,128)(2,1)}, u32[]{:S(2)}) copy-start(bf16[1,128,3584]{2,1,0:T(8,128)(2,1)} %param.17) | copy-start | bytes 2752516
  7.2 4.0 copy-start.7
  7.2 194.3 %all-gather.3.cloned.1.call-start = ((), (), s32[]{:S(2)}) async-start(), calls=%async_computation.3 | async-start | bytes 10321920 | tf_op jit(solution)/shard_map/all_gather | solution.py:75
  78.5 226.9 %all-gather.5.cloned.1.call-start = ((), (), s32[]{:S(2)}) async-start(), calls=%async_computation.4 | async-start | bytes 10321920 | tf_op jit(solution)/shard_map/all_gather | solution.py:76
  143.0 3.4 copy-start.2
  145.6 2.1 copy-start.3
  146.4 2.6 copy-start.9
  147.7 53.8 %copy-start.8 = (bf16[1,3584,128]{2,1,0:T(8,128)(2,1)S(1)}, bf16[1,3584,128]{2,1,0:T(8,128)(2,1)}, u32[]{:S(2)}) copy-start(bf16[1,3584,128]{2,1,0:T(8,128)(2,1)} %param.16) | copy-start | bytes 2752516
  207.6 105.2 %copy-start.5 = (bf16[1,3584,128]{1,2,0:T(8,128)(2,1)S(1)}, bf16[1,3584,128]{1,2,0:T(8,128)(2,1)}, u32[]{:S(2)}) copy-start(bf16[1,3584,128]{1,2,0:T(8,128)(2,1)} %copy.24) | copy-start | bytes 2752516
  207.7 105.2 %copy-start.6 = (bf16[1,3584,128]{1,2,0:T(8,128)(2,1)S(1)}, bf16[1,3584,128]{1,2,0:T(8,128)(2,1)}, u32[]{:S(2)}) copy-start(bf16[1,3584,128]{1,2,0:T(8,128)(2,1)} %copy.25) | copy-start | bytes 2752516
  334.6 10.1 %copy-start.4 = (bf16[1,3584,128]{1,2,0:T(8,128)(2,1)S(1)}, bf16[1,3584,128]{1,2,0:T(8,128)(2,1)}, u32[]{:S(2)}) copy-start(bf16[1,3584,128]{1,2,0:T(8,128)(2,1)} %get-tuple-element.16) | copy-start | bytes 2752516
  334.6 57.0 %all-to-all-start.2 = ((bf16[32,112,256]{2,1,0:T(8,128)(2,1)}), bf16[32,112,256]{2,1,0:T(8,128)(2,1)}, u32[]{:S(2)}, u32[]{:S(2)}) async-start(bf16[32,112,256]{2,1,0:T(8,128)(2,1)} %broadcast_select_fusion), calls=%async_computation.2 | async-start | bytes 3670016 | tf_op jit(solution)/shard_map/all_to_all | solution.py:88
  344.6 1.3 copy-start.1
Sparse Core Ops, SparseCore 0:
  78.6 122.7 all-gather.2
  203.3 102.1 all-gather.4
where the time goes:
time: 403 us; the launch traced here: 400 us
  waiting for transfers between devices  195 us (48%)
  blocking collectives  124 us (31%)
  matrix products  28.6 us (7%)
  local copies, waits for them, and re-layouts  19.5 us (5%)
  between operations  14.9 us (4%)
  starting transfers between devices  10.1 us (3%)
  other arithmetic  7.97 us (2%)
    all_gather x1, waiting for transfers between devices, on_device(): lax.all_gather(recv_c, 'dp', axis=0, tiled=True)  97.8 us
    all_to_all x1, blocking collectives, on_device(): lax.all_to_all(send_c, 'expert', split_axis=0, concat_axis=0, tiled=True)  62.8 us
    all_to_all x1, blocking collectives, on_device(): lax.all_to_all(send_x, 'expert', split_axis=0, concat_axis=0, tiled=True)  61 us
    all_gather x1, waiting for transfers between devices, on_device(): lax.all_gather(recv_x, 'dp', axis=0, tiled=True)  52.4 us
    all_to_all x1, waiting for transfers between devices, on_device(): lax.all_to_all(outgoing, 'expert', split_axis=0, concat_axis=0, tiled=True)  44.6 us
    dot_general x1, matrix products, expert_terms(): lax.dot_general(rows_x, pre_grad, (((0,), (0,)), ((), ())), preferred_ele...  14.3 us
    all_to_all x1, starting transfers between devices, on_device(): lax.all_to_all(outgoing, 'expert', split_axis=0, concat_axis=0, tiled=True)  10.1 us
  transfers between devices with their start and end apart: 3, of which 3 were waited for; matrix products, arithmetic and copies ran while one was open for 4% of the time, Pallas kernels for 0%

commit v1 on v0

v1 whole, which is shorter than its diff:
```python
import functools

import jax
import jax.numpy as jnp
from jax import lax
from jax.experimental import pallas as pl
from jax.experimental.pallas import tpu as pltpu
from jax.sharding import PartitionSpec as P

BETA_ONE = 0.9
BETA_TWO = 0.95
EPSILON = 1e-08

MESH = pl.DeviceIdType.MESH
F32 = jnp.float32
BF16 = jnp.bfloat16

SLOTS = 5
COLS = 16
SIDE = 4
HALF = 4
RING = 8
PARTS = 4
WIDTH = 256
MSG = PARTS * 2 * SLOTS
UNIT = COLS * SLOTS
ALL = COLS * MSG


def mul_t(a, b):
    return lax.dot_general(a, b, (((1,), (1,)), ((), ())), preferred_element_type=F32)


def mul(a, b):
    return lax.dot_general(a, b, (((1,), (0,)), ((), ())), preferred_element_type=F32)


def adam_step(gradient, moment_one, moment_two):
    new_one = BETA_ONE * moment_one.astype(F32) + (1.0 - BETA_ONE) * gradient
    new_two = BETA_TWO * moment_two.astype(F32) + (1.0 - BETA_TWO) * gradient * gradient
    return new_one / (jnp.sqrt(new_two) + EPSILON)


def kernel(
    routes_ref, gates_ref, tok_hbm, cot_hbm, wup_hbm, wdn_hbm, mup_hbm, vup_hbm, mdn_hbm, vdn_hbm,
    sup_hbm, sdn_hbm,
    tok, cot, wup, wdn, mup, vup, mdn, vdn, sup, sdn,
    pick, unpick, packed, landed, own, other, transit, gup, gdn,
    load_sem, out_sem, plane_send, plane_recv, plane_self,
    chain_send, chain_recv, other_send, transit_send, transit_recv, mate_send, mate_recv,
):
    chunks = packed.shape[0]
    half_width = tok.shape[1] // 2
    dp = lax.axis_index("dp")
    ex = lax.axis_index("expert")
    core = lax.rem(dp, 2)
    pos = dp // 2
    zhi = lax.rem(ex, 2)
    col = ex // 2
    cy, cx = col // SIDE, lax.rem(col, SIDE)
    z = zhi * HALF + pos
    me_other = 1 - zhi

    def at_z(z_to):
        return ((z_to % HALF) * 2 + core, col * 2 + z_to // HALF)

    znext, zprev = lax.rem(z + 1, RING), lax.rem(z + RING - 1, RING)
    mate = (pos * 2 + (1 - core), ex)

    def peer_col(i):
        return lax.rem(cy + i // SIDE, SIDE) * SIDE + lax.rem(cx + i % SIDE, SIDE)

    barrier = pltpu.get_barrier_semaphore()
    for i in range(1, COLS):
        pl.semaphore_signal(
            barrier, inc=1, device_id=(dp, peer_col(i) * 2 + zhi), device_id_type=MESH
        )
    for who in (at_z(znext), at_z(zprev), mate):
        pl.semaphore_signal(barrier, inc=1, device_id=who, device_id_type=MESH)

    loads = [
        pltpu.make_async_copy(src, dst, load_sem.at[i])
        for i, (src, dst) in enumerate(
            (
                (tok_hbm, tok),
                (cot_hbm, cot),
                (wup_hbm, wup),
                (wdn_hbm, wdn),
                (mup_hbm, mup),
                (vup_hbm, vup),
                (mdn_hbm, mdn),
                (vdn_hbm, vdn),
            )
        )
    ]
    for load in loads:
        load.start()

    count = tok.shape[0]
    routes = routes_ref[...]
    expert_ids = lax.broadcasted_iota(jnp.int32, (2 * COLS, count), 0)
    member = (expert_ids == routes).astype(F32)
    before = (
        lax.broadcasted_iota(jnp.int32, (count, count), 0)
        < lax.broadcasted_iota(jnp.int32, (count, count), 1)
    ).astype(BF16)
    rank = jnp.sum(member * mul(member.astype(BF16), before), axis=0, keepdims=True)
    place = (routes >> 1) * MSG + (routes & 1) * SLOTS + rank.astype(jnp.int32)
    eye = lax.broadcasted_iota(jnp.int32, (count, count), 0) == lax.broadcasted_iota(
        jnp.int32, (count, count), 1
    )
    gates = jnp.sum(
        jnp.where(eye, jnp.broadcast_to(gates_ref[...], (count, count)), 0.0), axis=1, keepdims=True
    )
    target = lax.broadcasted_iota(jnp.int32, (ALL, count), 0)
    for part in range(PARTS):
        pick[:, part * count : (part + 1) * count] = (target == place + part * 2 * SLOTS).astype(
            F32
        ).astype(BF16)

    line = lax.broadcasted_iota(jnp.int32, (UNIT, ALL), 0)
    source = lax.broadcasted_iota(jnp.int32, (UNIT, ALL), 1)
    fifth = (line * 205) >> 10
    base = fifth * MSG + (line - fifth * SLOTS)
    for part in range(PARTS):
        for which, half in ((0, zhi), (1, me_other)):
            start = (part * 2 + which) * UNIT
            unpick[start : start + UNIT, :] = (
                (source == base + (part * 2 * SLOTS + half * SLOTS)).astype(F32).astype(BF16)
            )

    gup[...] = jnp.zeros_like(gup)
    gdn[...] = jnp.zeros_like(gdn)

    pl.semaphore_wait(barrier, COLS - 1 + 3)
    loads[0].wait()
    loads[1].wait()

    def lanes(chunk, high):
        return pl.ds(pl.multiple_of(high * half_width + chunk * WIDTH, 128), WIDTH)

    def plane_copy(chunk, i):
        to = peer_col(i)
        return pltpu.make_async_remote_copy(
            src_ref=packed.at[chunk, to],
            dst_ref=landed.at[chunk, col],
            send_sem=plane_send.at[chunk, i],
            recv_sem=plane_recv.at[chunk, i],
            device_id=(dp, to * 2 + zhi),
            device_id_type=MESH,
        )

    def plane_keep(chunk):
        return pltpu.make_async_copy(
            packed.at[chunk, col], landed.at[chunk, col], plane_self.at[chunk]
        )

    @pl.loop(0, chunks)
    def _(chunk):
        both = [tok[:, lanes(chunk, h)] for h in range(2)]
        both += [
            (gates * cot[:, lanes(chunk, h)].astype(F32)).astype(BF16) for h in range(2)
        ]
        rows = mul(pick[...], jnp.concatenate(both, axis=0))
        packed[chunk] = rows.reshape(COLS, MSG, WIDTH).astype(BF16)
        plane_keep(chunk).start()

        @pl.loop(1, COLS)
        def _(i):
            plane_copy(chunk, i).start()

    def chain(slot, chunk, to_next, own_side):
        z_to = jnp.where(to_next, znext, zprev)
        return pltpu.make_async_remote_copy(
            src_ref=own.at[slot, core, chunk],
            dst_ref=own.at[slot, core, chunk],
            send_sem=chain_send.at[own_side, slot, chunk],
            recv_sem=chain_recv.at[slot, chunk],
            device_id=at_z(z_to),
            device_id_type=MESH,
        )

    def hand_over(slot, chunk):
        return pltpu.make_async_remote_copy(
            src_ref=own.at[slot, core, chunk],
            dst_ref=own.at[slot, core, chunk],
            send_sem=mate_send.at[slot, chunk],
            recv_sem=mate_recv.at[slot, chunk],
            device_id=mate,
            device_id_type=MESH,
        )

    upper = pos >= 2
    edge = (pos == 0) | (pos == HALF - 1)
    z_out = jnp.where(upper, znext, zprev)

    def other_inner(chunk):
        return pltpu.make_async_remote_copy(
            src_ref=other.at[chunk],
            dst_ref=transit.at[chunk],
            send_sem=other_send.at[chunk],
            recv_sem=transit_recv.at[chunk],
            device_id=at_z(z_out),
            device_id_type=MESH,
        )

    def other_edge(chunk):
        return pltpu.make_async_remote_copy(
            src_ref=other.at[chunk],
            dst_ref=own.at[z, core, chunk],
            send_sem=other_send.at[chunk],
            recv_sem=chain_recv.at[z, chunk],
            device_id=at_z(z_out),
            device_id_type=MESH,
        )

    z_via = jnp.where(upper, zprev, znext)

    def transit_edge(chunk):
        return pltpu.make_async_remote_copy(
            src_ref=transit.at[chunk],
            dst_ref=own.at[z_via, core, chunk],
            send_sem=transit_send.at[chunk],
            recv_sem=chain_recv.at[z_via, chunk],
            device_id=at_z(z_out),
            device_id_type=MESH,
        )

    @pl.loop(0, chunks)
    def _(chunk):
        plane_keep(chunk).wait()

        @pl.loop(1, COLS)
        def _(i):
            plane_copy(chunk, i).wait_recv()

        rows = mul(
            unpick[...], landed[chunk].astype(F32).reshape(ALL, WIDTH).astype(BF16)
        ).astype(BF16)
        for part in range(PARTS):
            start = part * 2 * UNIT
            own[z, core, chunk, :, part * WIDTH : (part + 1) * WIDTH] = rows[start : start + UNIT]
            other[chunk, :, part * WIDTH : (part + 1) * WIDTH] = rows[
                start + UNIT : start + 2 * UNIT
            ]

        @pl.when(edge)
        def _():
            other_edge(chunk).start()

        @pl.when(jnp.logical_not(edge))
        def _():
            other_inner(chunk).start()

        @pl.when(pos < HALF - 1)
        def _():
            chain(z, chunk, True, 1).start()

        @pl.when(pos > 0)
        def _():
            chain(z, chunk, False, 0).start()

        hand_over(z, chunk).start()

    for load in loads[2:]:
        load.wait()

    def pair(slot, chunk):
        return jnp.concatenate([own[slot, 0, chunk], own[slot, 1, chunk]], axis=0)

    def terms(slot):
        preact = jnp.zeros((2 * UNIT, wup.shape[1]), F32)
        back = jnp.zeros((2 * UNIT, wup.shape[1]), F32)
        for chunk in range(chunks):
            rows = pair(slot, chunk)
            for high in range(2):
                at = high * half_width + chunk * WIDTH
                preact += mul(
                    rows[:, high * WIDTH : (high + 1) * WIDTH], wup[at : at + WIDTH, :]
                )
                back += mul_t(
                    rows[:, (2 + high) * WIDTH : (3 + high) * WIDTH], wdn[:, at : at + WIDTH]
                )
        squash = jax.nn.sigmoid(preact)
        hidden = preact * squash
        pre_grad = back * (squash * (1.0 + preact * (1.0 - squash)))
        hidden = hidden.astype(BF16).astype(F32).T.astype(BF16)
        pre_grad = pre_grad.astype(BF16).astype(F32).T.astype(BF16)
        for chunk in range(chunks):
            rows = pair(slot, chunk)
            for high in range(2):
                at = high * half_width + chunk * WIDTH
                gup[:, at : at + WIDTH] += mul(
                    pre_grad, rows[:, high * WIDTH : (high + 1) * WIDTH]
                )
                gdn[:, at : at + WIDTH] += mul(
                    hidden, rows[:, (2 + high) * WIDTH : (3 + high) * WIDTH]
                )

    def finish(slot):
        @pl.loop(0, chunks)
        def _(chunk):
            hand_over(slot, chunk).wait_recv()

        terms(slot)

    @pl.when(edge)
    def _():
        @pl.loop(0, chunks)
        def _(chunk):
            other_inner(chunk).wait_recv()
            transit_edge(chunk).start()

    finish(z)

    @pl.loop(0, 10)
    def _(j):
        far = j // 2 + 1
        from_prev = (lax.rem(j, 2) == 1) == upper
        reach = jnp.where(from_prev, pos + 2, HALF + 1 - pos)

        @pl.when(far <= reach)
        def _():
            slot = lax.rem(jnp.where(from_prev, z + RING - far, z + far), RING)
            onward = jnp.where(from_prev, pos < HALF - 1, pos > 0)

            @pl.loop(0, chunks)
            def _(chunk):
                chain(slot, chunk, from_prev, 0).wait_recv()

                @pl.when(onward)
                def _():
                    chain(slot, chunk, from_prev, 0).start()

                hand_over(slot, chunk).start()

            finish(slot)

    model_width = tok.shape[1]
    block = 128

    @pl.loop(0, model_width // block)
    def _(b):
        at = pl.ds(pl.multiple_of(b * block, block), block)
        sup[at, :] = adam_step(gup[:, at].T, mup[at, :], vup[at, :]).astype(BF16)
        sdn[:, at] = adam_step(gdn[:, at], mdn[:, at], vdn[:, at]).astype(BF16)

    outs = [
        pltpu.make_async_copy(sup, sup_hbm, out_sem.at[0]),
        pltpu.make_async_copy(sdn, sdn_hbm, out_sem.at[1]),
    ]
    for out in outs:
        out.start()

    @pl.loop(0, chunks)
    def _(chunk):
        @pl.loop(1, COLS)
        def _(i):
            plane_copy(chunk, i).wait_send()

        other_inner(chunk).wait_send()
        hand_over(z, chunk).wait_send()

        @pl.when(edge)
        def _():
            transit_edge(chunk).wait_send()

        @pl.when(pos < HALF - 1)
        def _():
            chain(z, chunk, True, 1).wait_send()

        @pl.when(pos > 0)
        def _():
            chain(z, chunk, False, 0).wait_send()

    @pl.loop(0, 10)
    def _(j):
        far = j // 2 + 1
        from_prev = (lax.rem(j, 2) == 1) == upper
        reach = jnp.where(from_prev, pos + 2, HALF + 1 - pos)

        @pl.when(far <= reach)
        def _():
            slot = lax.rem(jnp.where(from_prev, z + RING - far, z + far), RING)
            onward = jnp.where(from_prev, pos < HALF - 1, pos > 0)

            @pl.loop(0, chunks)
            def _(chunk):
                @pl.when(onward)
                def _():
                    chain(slot, chunk, from_prev, 0).wait_send()

                hand_over(slot, chunk).wait_send()

    for out in outs:
        out.wait()


def expert_steps(routes, gates, tokens, cotangent, w_up, w_down, m_up, v_up, m_down, v_down):
    count, model_width = tokens.shape
    hidden = w_up.shape[1]
    chunks = model_width // 2 // WIDTH
    vmem = pl.BlockSpec(memory_space=pltpu.VMEM)
    anyw = pl.BlockSpec(memory_space=pl.ANY)
    dma = pltpu.SemaphoreType.DMA
    return pl.pallas_call(
        kernel,
        out_shape=(
            jax.ShapeDtypeStruct((model_width, hidden), BF16),
            jax.ShapeDtypeStruct((hidden, model_width), BF16),
        ),
        in_specs=[vmem, vmem] + [anyw] * 8,
        out_specs=(anyw, anyw),
        scratch_shapes=[
            pltpu.VMEM((count, model_width), BF16),
            pltpu.VMEM((count, model_width), BF16),
            pltpu.VMEM((model_width, hidden), BF16),
            pltpu.VMEM((hidden, model_width), BF16),
            pltpu.VMEM((model_width, hidden), BF16),
            pltpu.VMEM((model_width, hidden), BF16),
            pltpu.VMEM((hidden, model_width), BF16),
            pltpu.VMEM((hidden, model_width), BF16),
            pltpu.VMEM((model_width, hidden), BF16),
            pltpu.VMEM((hidden, model_width), BF16),
            pltpu.VMEM((ALL, PARTS * count), BF16),
            pltpu.VMEM((PARTS * 2 * UNIT, ALL), BF16),
            pltpu.VMEM((chunks, COLS, MSG, WIDTH), BF16),
            pltpu.VMEM((chunks, COLS, MSG, WIDTH), BF16),
            pltpu.VMEM((RING, 2, chunks, UNIT, PARTS * WIDTH), BF16),
            pltpu.VMEM((chunks, UNIT, PARTS * WIDTH), BF16),
            pltpu.VMEM((chunks, UNIT, PARTS * WIDTH), BF16),
            pltpu.VMEM((hidden, model_width), F32),
            pltpu.VMEM((hidden, model_width), F32),
            dma((8,)),
            dma((2,)),
            dma((chunks, COLS)),
            dma((chunks, COLS)),
            dma((chunks,)),
            dma((2, RING, chunks)),
            dma((RING, chunks)),
            dma((chunks,)),
            dma((chunks,)),
            dma((chunks,)),
            dma((RING, chunks)),
            dma((RING, chunks)),
        ],
        compiler_params=pltpu.CompilerParams(
            collective_id=0, has_side_effects=True, vmem_limit_bytes=60 * 1024 * 1024
        ),
        name="expert_steps",
    )(routes, gates, tokens, cotangent, w_up, w_down, m_up, v_up, m_down, v_down)


def on_device(
    tokens, cotangent, gates, routes, w_up, w_down, m_up, v_up, m_down, v_down, leaving, tile_owner
):
    experts = lax.axis_size("expert")
    my_index = lax.axis_index("expert")
    tok_count, model_width = tokens.shape
    hidden_units = w_up.shape[2]
    leaver = leaving[0]
    slot_ids = jnp.arange(experts, dtype=jnp.int32)
    tile_rows = model_width // experts
    adopt = jnp.sum(
        jnp.where(tile_owner[None, :] == slot_ids[:, None], slot_ids[None, :], 0), axis=1
    )
    step_up, step_down = expert_steps(
        routes.reshape(1, tok_count),
        gates.reshape(1, tok_count),
        tokens,
        cotangent,
        w_up[0],
        w_down[0],
        m_up[0],
        v_up[0],
        m_down[0],
        v_down[0],
    )
    keep_own = my_index != leaver
    both_steps = jnp.concatenate([step_up, step_down.T], axis=1).reshape(
        experts, tile_rows, 2 * hidden_units
    )
    ordered = both_steps[adopt]
    outgoing = jnp.where(keep_own, jnp.zeros_like(ordered), ordered)
    incoming = lax.all_to_all(outgoing, "expert", split_axis=0, concat_axis=0, tiled=True)
    mine = lax.dynamic_index_in_dim(incoming, leaver, 0, keepdims=False)
    adopted_up = mine[:, :hidden_units][None]
    adopted_down = mine[:, hidden_units:][None]
    update_up = jnp.where(keep_own, step_up, jnp.zeros_like(step_up))[None]
    update_down = jnp.where(keep_own, step_down, jnp.zeros_like(step_down))[None]
    return (update_up, update_down, adopted_up, adopted_down)


def solution(mesh):
    placed = (
        P(("dp", "expert"), None),
        P(("dp", "expert"), None),
        P(("dp", "expert"), None),
        P(("dp", "expert"), None),
        P("expert", None, "dp"),
        P("expert", "dp", None),
        P("expert", None, "dp"),
        P("expert", None, "dp"),
        P("expert", "dp", None),
        P("expert", "dp", None),
        P(),
        P(),
    )
    return jax.shard_map(
        on_device,
        mesh=mesh,
        in_specs=placed,
        out_specs=(
            P("expert", None, "dp"),
            P("expert", "dp", None),
            P("expert", None, "dp"),
            P("expert", None, "dp"),
        ),
        check_vma=False,
    )
```

time: 403 us -> 247 us (0.61)
  Pallas kernels: 0 us -> 181 us
  waiting for transfers between devices: 195 us -> 36.9 us
  blocking collectives: 124 us -> 0 us
  matrix products: 28.6 us -> 0 us
  between operations: 14.9 us -> 1.35 us
  local copies, waits for them, and re-layouts: 19.5 us -> 7.86 us
    pallas_call x0 -> x1, Pallas kernels: none -> 181 us  [expert_steps(): pl.pallas_call(kernel, out_shape=(jax.ShapeDtypeStruct((model_width, hidd...]
    all_gather x2 -> x0, waiting for transfers between devices: 150 us -> none  [the longest x1 97.8 us: on_device(): lax.all_gather(recv_c, 'dp', axis=0, tiled=True)]
    all_to_all x2 -> x0, blocking collectives: 124 us -> none  [the longest x1 62.8 us: on_device(): lax.all_to_all(send_c, 'expert', split_axis=0, concat_axis=0, tiled=True)]
    dot_general x4 -> x0, matrix products: 28.6 us -> none  [the longest x1 14.3 us: expert_terms(): lax.dot_general(rows_x, pre_grad, (((0,), (0,)), ((), ())), preferred_ele...]
    reshape x4 -> x0, local copies, waits for them, and re-layouts: 8.24 us -> none  [the longest x1 2.63 us: on_device(): recv_c = recv_c.reshape(experts * capacity, model_width)]
    all_to_all x1, waiting for transfers between devices: 44.6 us -> 36.9 us  [on_device(): lax.all_to_all(outgoing, 'expert', split_axis=0, concat_axis=0, tiled=True)]
  transfers between devices with their start and end apart: 3 -> 1, of which waited for: 3 -> 1; matrix products, arithmetic and copies ran while one was open for 4% -> 1% of each run, Pallas kernels for 0% -> 0%
where the time goes in v1:
time: 247 us; the launch traced here: 245 us
  Pallas kernels  181 us (73%)
  waiting for transfers between devices  36.9 us (15%)
  starting transfers between devices  12.1 us (5%)
  local copies, waits for them, and re-layouts  7.86 us (3%)
  other arithmetic  5.4 us (2%)
    pallas_call x1, Pallas kernels, expert_steps(): pl.pallas_call(kernel, out_shape=(jax.ShapeDtypeStruct((model_width, hidd...  181 us
    all_to_all x1, waiting for transfers between devices, on_device(): lax.all_to_all(outgoing, 'expert', split_axis=0, concat_axis=0, tiled=True)  36.9 us
    all_to_all x1, starting transfers between devices, on_device(): lax.all_to_all(outgoing, 'expert', split_axis=0, concat_axis=0, tiled=True)  12.1 us
  transfers between devices with their start and end apart: 1, of which 1 were waited for; matrix products, arithmetic and copies ran while one was open for 1% of the time, Pallas kernels for 0%

profile of v1, /device:TPU:24, one launch (start us, length us, event | category | flops | bytes accessed | tf_op | source)
XLA Modules:
  0.0 244.9 jit_solution(9362469845932677869)
XLA Ops:
  1.3 0.8 select_reduce_fusion
  2.1 181.3 %expert_steps.1 = (bf16[3584,128]{1,0:T(8,128)(2,1)}, bf16[128,3584]{1,0:T(8,128)(2,1)}) custom-call(s32[1,128]{1,0:T(1,128)} %bitcast.37, f32[1,128]{1,0:T(1,128)} %bitcast.38, bf16[128,3584]{1,0:T(8,128)(2,1)} %tok_hbm.1, bf16[128,3584]{1,0:T(8,128)(2,1)} %cot_hbm.1, bf16[3584,128]{1,0:T(8,128)(2,1)} %bitcast.31, bf16[128,3584]{1,0:T(8,128)(2,1)} %bitcast.32, ...), custom_call_target="tpu_custom_call" | custom-call | tf_op jit(solution)/shard_map/expert_steps/pallas_call | solution.py:406
  183.4 1.5 copy.20
  184.9 1.3 pad_maximum_fusion
  186.2 2.3 copy.21
  188.5 2.2 gather_fusion
  190.6 1.4 broadcast_select_fusion
  192.0 0.0 copy-start.1
  192.0 12.1 %all-to-all-start = ((bf16[32,112,256]{2,1,0:T(8,128)(2,1)}), bf16[32,112,256]{2,1,0:T(8,128)(2,1)}, u32[]{:S(2)}, u32[]{:S(2)}) async-start(bf16[32,112,256]{2,1,0:T(8,128)(2,1)} %broadcast_select_fusion), calls=%async_computation | async-start | bytes 3670016 | tf_op jit(solution)/shard_map/all_to_all | solution.py:485
  204.1 0.0 copy-start
  204.2 0.0 copy-done.1
  204.2 1.0 select_bitcast_fusion.1
  205.2 0.5 copy-done
  205.6 1.0 select_bitcast_fusion
  206.6 36.9 %all-to-all-done = bf16[32,112,256]{2,1,0:T(8,128)(2,1)} async-done(((bf16[32,112,256]{2,1,0:T(8,128)(2,1)}), bf16[32,112,256]{2,1,0:T(8,128)(2,1)}, u32[]{:S(2)}, u32[]{:S(2)}) %all-to-all-start) | async-done | bytes 1835040 | tf_op jit(solution)/shard_map/all_to_all | solution.py:485
  243.5 0.8 dynamic-slice_bitcast_fusion
  244.3 0.6 slice_bitcast_fusion
  (2 shorter events, 0.0 us)
Async XLA Ops:
  192.0 12.2 %copy-start.1 = (bf16[3584,128]{1,0:T(8,128)(2,1)S(1)}, bf16[3584,128]{1,0:T(8,128)(2,1)}, u32[]{:S(2)}) copy-start(bf16[3584,128]{1,0:T(8,128)(2,1)} %get-tuple-element.6) | copy-start | bytes 2752516
  192.0 51.5 %all-to-all-start = ((bf16[32,112,256]{2,1,0:T(8,128)(2,1)}), bf16[32,112,256]{2,1,0:T(8,128)(2,1)}, u32[]{:S(2)}, u32[]{:S(2)}) async-start(bf16[32,112,256]{2,1,0:T(8,128)(2,1)} %broadcast_select_fusion), calls=%async_computation | async-start | bytes 3670016 | tf_op jit(solution)/shard_map/all_to_all | solution.py:485
  204.1 1.5 copy-start

commit v2 on v1

--- a/solution.py
+++ b/solution.py
@@ -42,12 +42,14 @@
 
 
 def kernel(
-    routes_ref, gates_ref, tok_hbm, cot_hbm, wup_hbm, wdn_hbm, mup_hbm, vup_hbm, mdn_hbm, vdn_hbm,
-    sup_hbm, sdn_hbm,
+    leaving_ref, adopt_ref, routes_ref, gates_ref, tok_hbm, cot_hbm, wup_hbm, wdn_hbm, mup_hbm, vup_hbm, mdn_hbm, vdn_hbm,
+    sup_hbm, sdn_hbm, aup_ref, adn_ref,
     tok, cot, wup, wdn, mup, vup, mdn, vdn, sup, sdn,
     pick, unpick, packed, landed, own, other, transit, gup, gdn,
+    leave_up, leave_dn, by_tile, tiles, hop, got, summed, fin, last,
     load_sem, out_sem, plane_send, plane_recv, plane_self,
     chain_send, chain_recv, other_send, transit_send, transit_recv, mate_send, mate_recv,
+    hop_send, hop_recv, ring_send, ring_recv, fin_send, fin_recv, last_send, last_recv,
 ):
     chunks = packed.shape[0]
     half_width = tok.shape[1] // 2
@@ -75,7 +77,8 @@
         pl.semaphore_signal(
             barrier, inc=1, device_id=(dp, peer_col(i) * 2 + zhi), device_id_type=MESH
         )
-    for who in (at_z(znext), at_z(zprev), mate):
+    twin = (dp, col * 2 + me_other)
+    for who in (at_z(znext), at_z(zprev), mate, twin):
         pl.semaphore_signal(barrier, inc=1, device_id=who, device_id_type=MESH)
 
     loads = [
@@ -132,7 +135,7 @@
     gup[...] = jnp.zeros_like(gup)
     gdn[...] = jnp.zeros_like(gdn)
 
-    pl.semaphore_wait(barrier, COLS - 1 + 3)
+    pl.semaphore_wait(barrier, COLS - 1 + 4)
     loads[0].wait()
     loads[1].wait()
 
@@ -338,19 +341,139 @@
 
     model_width = tok.shape[1]
     block = 128
+    leaves = jnp.broadcast_to(leaving_ref[...], (block, block)) == ex
+    ring_at, line_at = (cx, cy), (cy, cx)
+    middle = SIDE
+
+    def tile_home(axis, ring_to, line_to):
+        to = line_to * SIDE + ring_to if axis == 0 else ring_to * SIDE + line_to
+        return (dp, to * 2 + zhi)
+
+    def ring_next(axis, far):
+        return lax.rem(ring_at[axis] + far, SIDE)
+
+    def ring_to(axis, side):
+        return tile_home(axis, ring_next(axis, 1 if side == 0 else SIDE - 1), line_at[axis])
+
+    def part_of(side):
+        return pl.ds(0, middle) if side == 0 else pl.ds(middle, middle)
+
+    def hop_copy(axis, side):
+        return pltpu.make_async_remote_copy(
+            src_ref=tiles.at[axis, ring_next(axis, 2), part_of(side)],
+            dst_ref=hop.at[axis, side],
+            send_sem=hop_send.at[axis, side],
+            recv_sem=hop_recv.at[axis, side],
+            device_id=ring_to(axis, side),
+            device_id_type=MESH,
+        )
+
+    def ring_copy(axis, side, late):
+        part = part_of(side if late else 1 - side)
+        return pltpu.make_async_remote_copy(
+            src_ref=tiles.at[axis, ring_next(axis, 1 if side == 0 else SIDE - 1), part],
+            dst_ref=got.at[axis, side, part],
+            send_sem=ring_send.at[axis, side, late],
+            recv_sem=ring_recv.at[axis, side, late],
+            device_id=ring_to(axis, side),
+            device_id_type=MESH,
+        )
+
+    def fin_copy(axis, far):
+        line_to = lax.rem(line_at[axis] + far, SIDE)
+        return pltpu.make_async_remote_copy(
+            src_ref=summed.at[axis, pl.ds(line_to * 2, 2)],
+            dst_ref=fin.at[axis, far - 1],
+            send_sem=fin_send.at[axis, far - 1],
+            recv_sem=fin_recv.at[axis, far - 1],
+            device_id=tile_home(axis, ring_at[axis], line_to),
+            device_id_type=MESH,
+        )
+
+    def last_copy(axis):
+        return pltpu.make_async_remote_copy(
+            src_ref=summed.at[axis, line_at[axis] * 2 + me_other],
+            dst_ref=last.at[axis],
+            send_sem=last_send.at[axis],
+            recv_sem=last_recv.at[axis],
+            device_id=twin,
+            device_id_type=MESH,
+        )
+
+    def sort_tiles(axis, leave):
+        rows = tiles.shape[3]
+        for tile in range(2 * COLS):
+            by_tile[tile] = leave[tile * rows : (tile + 1) * rows, :]
+
+        @pl.loop(0, 2 * COLS)
+        def _(owner):
+            to = owner // 2
+            ty, tx = to // SIDE, lax.rem(to, SIDE)
+            r, l = (tx, ty) if axis == 0 else (ty, tx)
+            tiles[axis, r, l * 2 + lax.rem(owner, 2)] = by_tile[adopt_ref[owner]]
+
+        for side in range(2):
+            hop_copy(axis, side).start()
+        for side in range(2):
+            ring_copy(axis, side, 0).start()
 
     @pl.loop(0, model_width // block)
     def _(b):
         at = pl.ds(pl.multiple_of(b * block, block), block)
-        sup[at, :] = adam_step(gup[:, at].T, mup[at, :], vup[at, :]).astype(BF16)
-        sdn[:, at] = adam_step(gdn[:, at], mdn[:, at], vdn[:, at]).astype(BF16)
-
-    outs = [
-        pltpu.make_async_copy(sup, sup_hbm, out_sem.at[0]),
-        pltpu.make_async_copy(sdn, sdn_hbm, out_sem.at[1]),
-    ]
-    for out in outs:
-        out.start()
+        step = adam_step(gup[:, at].T, mup[at, :], vup[at, :])
+        sup[at, :] = jnp.where(leaves, 0.0, step).astype(BF16)
+        leave_up[at, :] = jnp.where(leaves, step, 0.0).astype(BF16)
+
+    out_up = pltpu.make_async_copy(sup, sup_hbm, out_sem.at[0])
+    out_up.start()
+    sort_tiles(0, leave_up)
+
+    @pl.loop(0, model_width // block)
+    def _(b):
+        at = pl.ds(pl.multiple_of(b * block, block), block)
+        step = adam_step(gdn[:, at], mdn[:, at], vdn[:, at])
+        sdn[:, at] = jnp.where(leaves, 0.0, step).astype(BF16)
+        leave_dn[at, :] = jnp.where(leaves, step, 0.0).T.astype(BF16)
+
+    out_dn = pltpu.make_async_copy(sdn, sdn_hbm, out_sem.at[1])
+    out_dn.start()
+    sort_tiles(1, leave_dn)
+
+    for axis in range(2):
+        for side in range(2):
+            hop_copy(axis, side).wait_recv()
+            to = ring_next(axis, 1 if side == 0 else SIDE - 1)
+            part = part_of(side)
+            tiles[axis, to, part] = tiles[axis, to, part] + hop[axis, side]
+            ring_copy(axis, side, 1).start()
+
+    for axis in range(2):
+        for side in range(2):
+            for late in range(2):
+                ring_copy(axis, side, late).wait_recv()
+        summed[axis] = tiles[axis, ring_at[axis]] + got[axis, 0] + got[axis, 1]
+        for far in range(1, SIDE):
+            fin_copy(axis, far).start()
+
+    for axis in range(2):
+        for far in range(1, SIDE):
+            fin_copy(axis, far).wait_recv()
+        mine = pl.ds(line_at[axis] * 2, 2)
+        summed[axis, mine] = summed[axis, mine] + fin[axis, 0] + fin[axis, 1] + fin[axis, 2]
+        last_copy(axis).start()
+
+    for axis, adopted in ((0, aup_ref), (1, adn_ref)):
+        last_copy(axis).wait_recv()
+        adopted[...] = summed[axis, line_at[axis] * 2 + zhi] + last[axis]
+
+    for axis in range(2):
+        for side in range(2):
+            hop_copy(axis, side).wait_send()
+            for late in range(2):
+                ring_copy(axis, side, late).wait_send()
+        for far in range(1, SIDE):
+            fin_copy(axis, far).wait_send()
+        last_copy(axis).wait_send()
 
     @pl.loop(0, chunks)
     def _(chunk):
@@ -392,14 +515,16 @@
 
                 hand_over(slot, chunk).wait_send()
 
-    for out in outs:
-        out.wait()
-
-
-def expert_steps(routes, gates, tokens, cotangent, w_up, w_down, m_up, v_up, m_down, v_down):
+    out_up.wait()
+    out_dn.wait()
+
+
+def expert_steps(leaving, adopt, routes, gates, tokens, cotangent, w_up, w_down, m_up, v_up, m_down, v_down):
     count, model_width = tokens.shape
     hidden = w_up.shape[1]
     chunks = model_width // 2 // WIDTH
+    tile_rows = model_width // adopt.shape[0]
+    smem = pl.BlockSpec(memory_space=pltpu.SMEM)
     vmem = pl.BlockSpec(memory_space=pltpu.VMEM)
     anyw = pl.BlockSpec(memory_space=pl.ANY)
     dma = pltpu.SemaphoreType.DMA
@@ -408,9 +533,11 @@
         out_shape=(
             jax.ShapeDtypeStruct((model_width, hidden), BF16),
             jax.ShapeDtypeStruct((hidden, model_width), BF16),
+            jax.ShapeDtypeStruct((tile_rows, hidden), BF16),
+            jax.ShapeDtypeStruct((tile_rows, hidden), BF16),
         ),
-        in_specs=[vmem, vmem] + [anyw] * 8,
-        out_specs=(anyw, anyw),
+        in_specs=[vmem, smem, vmem, vmem] + [anyw] * 8,
+        out_specs=(anyw, anyw, vmem, vmem),
         scratch_shapes=[
             pltpu.VMEM((count, model_width), BF16),
             pltpu.VMEM((count, model_width), BF16),
@@ -431,6 +558,15 @@
             pltpu.VMEM((chunks, UNIT, PARTS * WIDTH), BF16),
             pltpu.VMEM((hidden, model_width), F32),
             pltpu.VMEM((hidden, model_width), F32),
+            pltpu.VMEM((model_width, hidden), BF16),
+            pltpu.VMEM((model_width, hidden), BF16),
+            pltpu.VMEM((2 * COLS, tile_rows, hidden), BF16),
+            pltpu.VMEM((2, SIDE, 2 * SIDE, tile_rows, hidden), BF16),
+            pltpu.VMEM((2, 2, SIDE, tile_rows, hidden), BF16),
+            pltpu.VMEM((2, 2, 2 * SIDE, tile_rows, hidden), BF16),
+            pltpu.VMEM((2, 2 * SIDE, tile_rows, hidden), BF16),
+            pltpu.VMEM((2, SIDE - 1, 2, tile_rows, hidden), BF16),
+            pltpu.VMEM((2, tile_rows, hidden), BF16),
             dma((8,)),
             dma((2,)),
             dma((chunks, COLS)),
@@ -443,28 +579,34 @@
             dma((chunks,)),
             dma((RING, chunks)),
             dma((RING, chunks)),
+            dma((2, 2)),
+            dma((2, 2)),
+            dma((2, 2, 2)),
+            dma((2, 2, 2)),
+            dma((2, SIDE - 1)),
+            dma((2, SIDE - 1)),
+            dma((2,)),
+            dma((2,)),
         ],
         compiler_params=pltpu.CompilerParams(
             collective_id=0, has_side_effects=True, vmem_limit_bytes=60 * 1024 * 1024
         ),
         name="expert_steps",
-    )(routes, gates, tokens, cotangent, w_up, w_down, m_up, v_up, m_down, v_down)
+    )(leaving, adopt, routes, gates, tokens, cotangent, w_up, w_down, m_up, v_up, m_down, v_down)
 
 
 def on_device(
     tokens, cotangent, gates, routes, w_up, w_down, m_up, v_up, m_down, v_down, leaving, tile_owner
 ):
     experts = lax.axis_size("expert")
-    my_index = lax.axis_index("expert")
-    tok_count, model_width = tokens.shape
-    hidden_units = w_up.shape[2]
-    leaver = leaving[0]
+    tok_count = tokens.shape[0]
     slot_ids = jnp.arange(experts, dtype=jnp.int32)
-    tile_rows = model_width // experts
     adopt = jnp.sum(
         jnp.where(tile_owner[None, :] == slot_ids[:, None], slot_ids[None, :], 0), axis=1
     )
-    step_up, step_down = expert_steps(
+    outs = expert_steps(
+        leaving.reshape(1, 1),
+        adopt,
         routes.reshape(1, tok_count),
         gates.reshape(1, tok_count),
         tokens,
@@ -476,19 +618,7 @@
         m_down[0],
         v_down[0],
     )
-    keep_own = my_index != leaver
-    both_steps = jnp.concatenate([step_up, step_down.T], axis=1).reshape(
-        experts, tile_rows, 2 * hidden_units
-    )
-    ordered = both_steps[adopt]
-    outgoing = jnp.where(keep_own, jnp.zeros_like(ordered), ordered)
-    incoming = lax.all_to_all(outgoing, "expert", split_axis=0, concat_axis=0, tiled=True)
-    mine = lax.dynamic_index_in_dim(incoming, leaver, 0, keepdims=False)
-    adopted_up = mine[:, :hidden_units][None]
-    adopted_down = mine[:, hidden_units:][None]
-    update_up = jnp.where(keep_own, step_up, jnp.zeros_like(step_up))[None]
-    update_down = jnp.where(keep_own, step_down, jnp.zeros_like(step_down))[None]
-    return (update_up, update_down, adopted_up, adopted_down)
+    return tuple(out[None] for out in outs)
 
 
 def solution(mesh):

time: 247 us -> 219 us (0.89)
  waiting for transfers between devices: 36.9 us -> 0 us
  Pallas kernels: 181 us -> 212 us
  starting transfers between devices: 12.1 us -> 0 us
  other arithmetic: 5.4 us -> 0.63 us
  local copies, waits for them, and re-layouts: 7.86 us -> 5.19 us
    all_to_all x1 -> x0, waiting for transfers between devices: 36.9 us -> none  [on_device(): lax.all_to_all(outgoing, 'expert', split_axis=0, concat_axis=0, tiled=True)]
    pallas_call x1, Pallas kernels: 181 us -> 212 us  [expert_steps(): pl.pallas_call(kernel, out_shape=(jax.ShapeDtypeStruct((model_width, hidd...]
    all_to_all x1 -> x0, starting transfers between devices: 12.1 us -> none  [on_device(): lax.all_to_all(outgoing, 'expert', split_axis=0, concat_axis=0, tiled=True)]
    unnamed x4 -> x12, local copies, waits for them, and re-layouts: 0.5 us -> 5.19 us
  transfers between devices with their start and end apart: 1 -> 0, of which waited for: 1 -> 0; matrix products, arithmetic and copies ran while one was open for 1% -> 0% of each run, Pallas kernels for 0% -> 0%
where the time goes in v2:
time: 219 us
  Pallas kernels  212 us (97%)
  local copies, waits for them, and re-layouts  5.19 us (2%)
    pallas_call x1, Pallas kernels, expert_steps(): pl.pallas_call(kernel, out_shape=(jax.ShapeDtypeStruct((model_width, hidd...  212 us
    unnamed x12, local copies, waits for them, and re-layouts  5.19 us

profile of v2, /device:TPU:24, one launch (start us, length us, event | category | flops | bytes accessed | tf_op | source)
XLA Modules:
  0.0 218.7 jit_solution(17024095128697938648)
XLA Ops:
  1.3 0.0 copy-start.3
  1.3 0.6 copy-done.3
  1.9 0.6 select_reduce_fusion.adopt_ref
  2.6 211.6 %expert_steps.1 = (bf16[3584,128]{1,0:T(8,128)(2,1)}, bf16[128,3584]{1,0:T(8,128)(2,1)}, bf16[112,128]{1,0:T(8,128)(2,1)}, bf16[112,128]{1,0:T(8,128)(2,1)}) custom-call(s32[1,1]{1,0:T(1,128)} %bitcast.13.leaving_ref, s32[32]{0:T(128)} %select_reduce_fusion.adopt_ref, s32[1,128]{1,0:T(1,128)} %bitcast.24, f32[1,128]{1,0:T(1,128)} %bitcast.25, ...), custom_call_target="tpu_custom_call" | custom-call | tf_op jit(solution)/shard_map/expert_steps/pallas_call | solution.py:531
  214.1 0.0 copy-start
  214.1 2.2 %copy.21 = bf16[1,3584,128]{2,1,0:T(8,128)(2,1)} copy(bf16[1,3584,128]{2,1,0:T(8,128)(2,1)} %bitcast.15) | data formatting | bytes 1835008
  216.4 0.0 copy-done
  216.4 0.0 copy-start.2
  216.4 0.9 copy.22
  217.3 0.0 copy-done.2
  217.3 0.0 copy-start.1
  217.3 0.6 copy.23
  217.9 0.1 copy-done.1
  218.1 0.6 copy.24
Async XLA Ops:
  1.3 0.7 copy-start.3
  214.1 2.3 %copy-start = (bf16[128,3584]{1,0:T(8,128)(2,1)S(1)}, bf16[128,3584]{1,0:T(8,128)(2,1)}, u32[]{:S(2)}) copy-start(bf16[128,3584]{1,0:T(8,128)(2,1)} %get-tuple-element.9) | copy-start | bytes 2752516
  216.4 0.9 copy-start.2
  217.3 0.8 copy-start.1

commit v3 on v2

--- a/solution.py
+++ b/solution.py
@@ -44,12 +44,12 @@
 def kernel(
     leaving_ref, adopt_ref, routes_ref, gates_ref, tok_hbm, cot_hbm, wup_hbm, wdn_hbm, mup_hbm, vup_hbm, mdn_hbm, vdn_hbm,
     sup_hbm, sdn_hbm, aup_ref, adn_ref,
-    tok, cot, wup, wdn, mup, vup, mdn, vdn, sup, sdn,
-    pick, unpick, packed, landed, own, other, transit, gup, gdn,
+    tok, cot, wup, wdn, wup_ward, wdn_ward, mup, vup, mdn, vdn, sup, sdn,
+    pick, unpick, packed, landed, own, other, transit, gup, gdn, pg_out, pg_in, gd_out, gd_in,
     leave_up, leave_dn, by_tile, tiles, hop, got, summed, fin, last,
     load_sem, out_sem, plane_send, plane_recv, plane_self,
     chain_send, chain_recv, other_send, transit_send, transit_recv, mate_send, mate_recv,
-    hop_send, hop_recv, ring_send, ring_recv, fin_send, fin_recv, last_send, last_recv,
+    ward_send, ward_recv, pg_send, pg_recv, gd_send, gd_recv, hop_send, hop_recv, ring_send, ring_recv, fin_send, fin_recv, last_send, last_recv,
 ):
     chunks = packed.shape[0]
     half_width = tok.shape[1] // 2
@@ -121,6 +121,67 @@
             F32
         ).astype(BF16)
 
+    pl.semaphore_wait(barrier, COLS - 1 + 4)
+
+    upper = pos >= 2
+    edge = (pos == 0) | (pos == HALF - 1)
+    inner = jnp.logical_not(edge)
+    out_sign = jnp.where(upper, 1, -1)
+    z_out = lax.rem(z + RING + out_sign, RING)
+    z_in = lax.rem(z + RING - out_sign, RING)
+
+    def ward_weights(i):
+        src, dst = ((wup_hbm, wup_ward), (wdn_hbm, wdn_ward))[i]
+        return pltpu.make_async_remote_copy(
+            src_ref=src,
+            dst_ref=dst,
+            send_sem=ward_send.at[i],
+            recv_sem=ward_recv.at[i],
+            device_id=at_z(z_in),
+            device_id_type=MESH,
+        )
+
+    @pl.when(edge)
+    def _():
+        for i in range(2):
+            ward_weights(i).start()
+
+    loads[0].wait()
+    loads[1].wait()
+
+    def lanes(chunk, high):
+        return pl.ds(pl.multiple_of(high * half_width + chunk * WIDTH, 128), WIDTH)
+
+    def plane_copy(chunk, i):
+        to = peer_col(i)
+        return pltpu.make_async_remote_copy(
+            src_ref=packed.at[chunk, to],
+            dst_ref=landed.at[chunk, col],
+            send_sem=plane_send.at[chunk, i],
+            recv_sem=plane_recv.at[chunk, i],
+            device_id=(dp, to * 2 + zhi),
+            device_id_type=MESH,
+        )
+
+    def plane_keep(chunk):
+        return pltpu.make_async_copy(
+            packed.at[chunk, col], landed.at[chunk, col], plane_self.at[chunk]
+        )
+
+    @pl.loop(0, chunks)
+    def _(chunk):
+        both = [tok[:, lanes(chunk, h)] for h in range(2)]
+        both += [
+            (gates * cot[:, lanes(chunk, h)].astype(F32)).astype(BF16) for h in range(2)
+        ]
+        rows = mul(pick[...], jnp.concatenate(both, axis=0))
+        packed[chunk] = rows.reshape(COLS, MSG, WIDTH).astype(BF16)
+        plane_keep(chunk).start()
+
+        @pl.loop(1, COLS)
+        def _(i):
+            plane_copy(chunk, i).start()
+
     line = lax.broadcasted_iota(jnp.int32, (UNIT, ALL), 0)
     source = lax.broadcasted_iota(jnp.int32, (UNIT, ALL), 1)
     fifth = (line * 205) >> 10
@@ -135,55 +196,27 @@
     gup[...] = jnp.zeros_like(gup)
     gdn[...] = jnp.zeros_like(gdn)
 
-    pl.semaphore_wait(barrier, COLS - 1 + 4)
-    loads[0].wait()
-    loads[1].wait()
-
-    def lanes(chunk, high):
-        return pl.ds(pl.multiple_of(high * half_width + chunk * WIDTH, 128), WIDTH)
-
-    def plane_copy(chunk, i):
-        to = peer_col(i)
-        return pltpu.make_async_remote_copy(
-            src_ref=packed.at[chunk, to],
-            dst_ref=landed.at[chunk, col],
-            send_sem=plane_send.at[chunk, i],
-            recv_sem=plane_recv.at[chunk, i],
-            device_id=(dp, to * 2 + zhi),
-            device_id_type=MESH,
-        )
-
-    def plane_keep(chunk):
-        return pltpu.make_async_copy(
-            packed.at[chunk, col], landed.at[chunk, col], plane_self.at[chunk]
-        )
-
-    @pl.loop(0, chunks)
-    def _(chunk):
-        both = [tok[:, lanes(chunk, h)] for h in range(2)]
-        both += [
-            (gates * cot[:, lanes(chunk, h)].astype(F32)).astype(BF16) for h in range(2)
-        ]
-        rows = mul(pick[...], jnp.concatenate(both, axis=0))
-        packed[chunk] = rows.reshape(COLS, MSG, WIDTH).astype(BF16)
-        plane_keep(chunk).start()
-
-        @pl.loop(1, COLS)
-        def _(i):
-            plane_copy(chunk, i).start()
-
-    def chain(slot, chunk, to_next, own_side):
-        z_to = jnp.where(to_next, znext, zprev)
+    def chain_full(slot, chunk, sem):
         return pltpu.make_async_remote_copy(
             src_ref=own.at[slot, core, chunk],
             dst_ref=own.at[slot, core, chunk],
-            send_sem=chain_send.at[own_side, slot, chunk],
+            send_sem=chain_send.at[sem, slot, chunk],
             recv_sem=chain_recv.at[slot, chunk],
-            device_id=at_z(z_to),
-            device_id_type=MESH,
-        )
-
-    def hand_over(slot, chunk):
+            device_id=at_z(z_in),
+            device_id_type=MESH,
+        )
+
+    def chain_thin(slot, chunk, sem):
+        return pltpu.make_async_remote_copy(
+            src_ref=own.at[slot, core, chunk, 0],
+            dst_ref=own.at[slot, core, chunk, 0],
+            send_sem=chain_send.at[sem, slot, chunk],
+            recv_sem=chain_recv.at[slot, chunk],
+            device_id=at_z(z_out),
+            device_id_type=MESH,
+        )
+
+    def hand_full(slot, chunk):
         return pltpu.make_async_remote_copy(
             src_ref=own.at[slot, core, chunk],
             dst_ref=own.at[slot, core, chunk],
@@ -193,9 +226,15 @@
             device_id_type=MESH,
         )
 
-    upper = pos >= 2
-    edge = (pos == 0) | (pos == HALF - 1)
-    z_out = jnp.where(upper, znext, zprev)
+    def hand_thin(slot, chunk):
+        return pltpu.make_async_remote_copy(
+            src_ref=own.at[slot, core, chunk, 0],
+            dst_ref=own.at[slot, core, chunk, 0],
+            send_sem=mate_send.at[slot, chunk],
+            recv_sem=mate_recv.at[slot, chunk],
+            device_id=mate,
+            device_id_type=MESH,
+        )
 
     def other_inner(chunk):
         return pltpu.make_async_remote_copy(
@@ -217,14 +256,32 @@
             device_id_type=MESH,
         )
 
-    z_via = jnp.where(upper, zprev, znext)
-
     def transit_edge(chunk):
         return pltpu.make_async_remote_copy(
             src_ref=transit.at[chunk],
-            dst_ref=own.at[z_via, core, chunk],
+            dst_ref=own.at[z_in, core, chunk],
             send_sem=transit_send.at[chunk],
-            recv_sem=chain_recv.at[z_via, chunk],
+            recv_sem=chain_recv.at[z_in, chunk],
+            device_id=at_z(z_out),
+            device_id_type=MESH,
+        )
+
+    def pg_copy(slot):
+        return pltpu.make_async_remote_copy(
+            src_ref=pg_out.at[slot],
+            dst_ref=pg_in.at[slot],
+            send_sem=pg_send.at[slot],
+            recv_sem=pg_recv.at[slot],
+            device_id=at_z(z_out),
+            device_id_type=MESH,
+        )
+
+    def gd_copy(b):
+        return pltpu.make_async_remote_copy(
+            src_ref=gd_out.at[b],
+            dst_ref=gd_in.at[b],
+            send_sem=gd_send.at[b],
+            recv_sem=gd_recv.at[b],
             device_id=at_z(z_out),
             device_id_type=MESH,
         )
@@ -242,70 +299,105 @@
         ).astype(BF16)
         for part in range(PARTS):
             start = part * 2 * UNIT
-            own[z, core, chunk, :, part * WIDTH : (part + 1) * WIDTH] = rows[start : start + UNIT]
-            other[chunk, :, part * WIDTH : (part + 1) * WIDTH] = rows[
-                start + UNIT : start + 2 * UNIT
-            ]
+            kind, high = part // 2, part % 2
+            at = slice(high * WIDTH, (high + 1) * WIDTH)
+            own[z, core, chunk, kind, :, at] = rows[start : start + UNIT]
+            other[chunk, kind, :, at] = rows[start + UNIT : start + 2 * UNIT]
 
         @pl.when(edge)
         def _():
             other_edge(chunk).start()
-
-        @pl.when(jnp.logical_not(edge))
+            chain_full(z, chunk, 0).start()
+            hand_thin(z, chunk).start()
+
+        @pl.when(inner)
         def _():
             other_inner(chunk).start()
-
-        @pl.when(pos < HALF - 1)
-        def _():
-            chain(z, chunk, True, 1).start()
-
-        @pl.when(pos > 0)
-        def _():
-            chain(z, chunk, False, 0).start()
-
-        hand_over(z, chunk).start()
+            chain_full(z, chunk, 0).start()
+            chain_thin(z, chunk, 1).start()
+            hand_full(z, chunk).start()
 
     for load in loads[2:]:
         load.wait()
 
-    def pair(slot, chunk):
-        return jnp.concatenate([own[slot, 0, chunk], own[slot, 1, chunk]], axis=0)
-
-    def terms(slot):
-        preact = jnp.zeros((2 * UNIT, wup.shape[1]), F32)
-        back = jnp.zeros((2 * UNIT, wup.shape[1]), F32)
+    hidden_units = wup.shape[1]
+
+    def pair(slot, chunk, kind, high):
+        at = slice(high * WIDTH, (high + 1) * WIDTH)
+        return jnp.concatenate(
+            [own[slot, 0, chunk, kind, :, at], own[slot, 1, chunk, kind, :, at]], axis=0
+        )
+
+    def places():
         for chunk in range(chunks):
-            rows = pair(slot, chunk)
             for high in range(2):
-                at = high * half_width + chunk * WIDTH
-                preact += mul(
-                    rows[:, high * WIDTH : (high + 1) * WIDTH], wup[at : at + WIDTH, :]
-                )
-                back += mul_t(
-                    rows[:, (2 + high) * WIDTH : (3 + high) * WIDTH], wdn[:, at : at + WIDTH]
-                )
+                yield chunk, high, high * half_width + chunk * WIDTH
+
+    def terms_inner(slot):
+        @pl.loop(0, chunks)
+        def _(chunk):
+            hand_full(slot, chunk).wait_recv()
+
+        preact = jnp.zeros((2 * UNIT, 2 * hidden_units), F32)
+        back = jnp.zeros((2 * UNIT, 2 * hidden_units), F32)
+        for chunk, high, at in places():
+            here = slice(at, at + WIDTH)
+            preact += mul(
+                pair(slot, chunk, 0, high),
+                jnp.concatenate([wup[here, :], wup_ward[here, :]], axis=1),
+            )
+            back += mul_t(
+                pair(slot, chunk, 1, high),
+                jnp.concatenate([wdn[:, here], wdn_ward[:, here]], axis=0),
+            )
         squash = jax.nn.sigmoid(preact)
         hidden = preact * squash
-        pre_grad = back * (squash * (1.0 + preact * (1.0 - squash)))
+        pre_grad = (back * (squash * (1.0 + preact * (1.0 - squash)))).astype(BF16)
+        pg_out[slot] = pre_grad[:, hidden_units:]
         hidden = hidden.astype(BF16).astype(F32).T.astype(BF16)
-        pre_grad = pre_grad.astype(BF16).astype(F32).T.astype(BF16)
-        for chunk in range(chunks):
-            rows = pair(slot, chunk)
-            for high in range(2):
-                at = high * half_width + chunk * WIDTH
-                gup[:, at : at + WIDTH] += mul(
-                    pre_grad, rows[:, high * WIDTH : (high + 1) * WIDTH]
-                )
-                gdn[:, at : at + WIDTH] += mul(
-                    hidden, rows[:, (2 + high) * WIDTH : (3 + high) * WIDTH]
-                )
-
-    def finish(slot):
+        pre_grad = pre_grad[:, :hidden_units].astype(F32).T.astype(BF16)
+        pg_copy(slot).start()
+        for chunk, high, at in places():
+            here = slice(at, at + WIDTH)
+            gdn[:, here] += mul(hidden, pair(slot, chunk, 1, high))
+            gup[:, here] += mul(pre_grad, pair(slot, chunk, 0, high))
+
+    def terms_edge(slot):
         @pl.loop(0, chunks)
         def _(chunk):
-            hand_over(slot, chunk).wait_recv()
-
-        terms(slot)
+            hand_thin(slot, chunk).wait_recv()
+
+        pg_copy(slot).wait_recv()
+        pre_grad = pg_in[slot].astype(F32).T.astype(BF16)
+        for chunk, high, at in places():
+            gup[:, at : at + WIDTH] += mul(pre_grad, pair(slot, chunk, 0, high))
+
+    def toward_out(far):
+        return lax.rem(z + RING + out_sign * far, RING)
+
+    def relay_out(far, chunk):
+        slot = toward_out(far)
+        chain_full(slot, chunk, 0).wait_recv()
+        chain_full(slot, chunk, 0).start()
+
+        @pl.when(edge)
+        def _():
+            hand_thin(slot, chunk).start()
+
+        @pl.when(inner)
+        def _():
+            hand_full(slot, chunk).start()
+
+    def relay_in(far, chunk):
+        slot = toward_out(-far)
+        chain_full(slot, chunk, 0).wait_recv()
+        chain_thin(slot, chunk, 0).start()
+        hand_full(slot, chunk).start()
+
+    def edge_unit(i):
+        thin = (i == 0) | (lax.rem(i, 2) == 1)
+        far = jnp.where(i == 0, 1, (i + 3) // 2)
+        return thin, toward_out(jnp.where(thin, -far, i // 2 - 1))
 
     @pl.when(edge)
     def _():
@@ -313,31 +405,54 @@
         def _(chunk):
             other_inner(chunk).wait_recv()
             transit_edge(chunk).start()
-
-    finish(z)
-
-    @pl.loop(0, 10)
-    def _(j):
-        far = j // 2 + 1
-        from_prev = (lax.rem(j, 2) == 1) == upper
-        reach = jnp.where(from_prev, pos + 2, HALF + 1 - pos)
-
-        @pl.when(far <= reach)
-        def _():
-            slot = lax.rem(jnp.where(from_prev, z + RING - far, z + far), RING)
-            onward = jnp.where(from_prev, pos < HALF - 1, pos > 0)
-
+            relay_out(1, chunk)
+
+        @pl.loop(0, chunks)
+        def _(chunk):
+            relay_out(2, chunk)
+
+        @pl.loop(0, RING)
+        def _(i):
+            thin, slot = edge_unit(i)
+
+            @pl.when(thin)
+            def _():
+                @pl.loop(0, chunks)
+                def _(chunk):
+                    chain_thin(slot, chunk, 0).wait_recv()
+                    hand_thin(slot, chunk).start()
+
+            terms_edge(slot)
+
+    @pl.when(inner)
+    def _():
+        @pl.loop(0, chunks)
+        def _(chunk):
+            relay_in(1, chunk)
+
+        for i in range(2):
+            ward_weights(i).wait_recv()
+
+        @pl.loop(1, HALF)
+        def _(k):
             @pl.loop(0, chunks)
             def _(chunk):
-                chain(slot, chunk, from_prev, 0).wait_recv()
-
-                @pl.when(onward)
+                relay_out(k, chunk)
+                relay_in(k + 1, chunk)
+                first = chunk == 2
+
+                @pl.when(first | (chunk == 5))
                 def _():
-                    chain(slot, chunk, from_prev, 0).start()
-
-                hand_over(slot, chunk).start()
-
-            finish(slot)
+                    terms_inner(toward_out(jnp.where(first, k - 1, -k)))
+
+        @pl.loop(0, 2)
+        def _(i):
+            terms_inner(toward_out(jnp.where(i == 0, HALF - 1, -HALF)))
+
+        span = gd_out.shape[2]
+        for b in range(gd_out.shape[0]):
+            gd_out[b] = gdn[hidden_units:, b * span : (b + 1) * span].astype(BF16)
+            gd_copy(b).start()
 
     model_width = tok.shape[1]
     block = 128
@@ -428,24 +543,36 @@
     out_up.start()
     sort_tiles(0, leave_up)
 
-    @pl.loop(0, model_width // block)
-    def _(b):
-        at = pl.ds(pl.multiple_of(b * block, block), block)
-        step = adam_step(gdn[:, at], mdn[:, at], vdn[:, at])
-        sdn[:, at] = jnp.where(leaves, 0.0, step).astype(BF16)
-        leave_dn[at, :] = jnp.where(leaves, step, 0.0).T.astype(BF16)
-
-    out_dn = pltpu.make_async_copy(sdn, sdn_hbm, out_sem.at[1])
-    out_dn.start()
-    sort_tiles(1, leave_dn)
-
-    for axis in range(2):
+    def pass_on(axis):
         for side in range(2):
             hop_copy(axis, side).wait_recv()
             to = ring_next(axis, 1 if side == 0 else SIDE - 1)
             part = part_of(side)
             tiles[axis, to, part] = tiles[axis, to, part] + hop[axis, side]
             ring_copy(axis, side, 1).start()
+
+    pass_on(0)
+    span = gd_in.shape[2]
+
+    @pl.loop(0, gd_in.shape[0])
+    def _(b):
+        @pl.when(edge)
+        def _():
+            gd_copy(b).wait_recv()
+            gdn[0:hidden_units, pl.ds(pl.multiple_of(b * span, block), span)] = gd_in[b].astype(F32)
+
+        @pl.loop(0, span // block)
+        def _(i):
+            at = pl.ds(pl.multiple_of(b * span + i * block, block), block)
+            step = adam_step(gdn[0:hidden_units, at], mdn[:, at], vdn[:, at])
+            sdn[:, at] = jnp.where(leaves, 0.0, step).astype(BF16)
+            leave_dn[at, :] = jnp.where(leaves, step, 0.0).T.astype(BF16)
+
+    out_dn = pltpu.make_async_copy(sdn, sdn_hbm, out_sem.at[1])
+    out_dn.start()
+    sort_tiles(1, leave_dn)
+
+    pass_on(1)
 
     for axis in range(2):
         for side in range(2):
@@ -482,38 +609,51 @@
             plane_copy(chunk, i).wait_send()
 
         other_inner(chunk).wait_send()
-        hand_over(z, chunk).wait_send()
+        chain_full(z, chunk, 0).wait_send()
 
         @pl.when(edge)
         def _():
             transit_edge(chunk).wait_send()
-
-        @pl.when(pos < HALF - 1)
+            hand_thin(z, chunk).wait_send()
+
+            @pl.loop(1, 3)
+            def _(far):
+                chain_full(toward_out(far), chunk, 0).wait_send()
+                hand_thin(toward_out(far), chunk).wait_send()
+
+            @pl.loop(1, 6)
+            def _(far):
+                hand_thin(toward_out(-far), chunk).wait_send()
+
+        @pl.when(inner)
         def _():
-            chain(z, chunk, True, 1).wait_send()
-
-        @pl.when(pos > 0)
-        def _():
-            chain(z, chunk, False, 0).wait_send()
-
-    @pl.loop(0, 10)
-    def _(j):
-        far = j // 2 + 1
-        from_prev = (lax.rem(j, 2) == 1) == upper
-        reach = jnp.where(from_prev, pos + 2, HALF + 1 - pos)
-
-        @pl.when(far <= reach)
-        def _():
-            slot = lax.rem(jnp.where(from_prev, z + RING - far, z + far), RING)
-            onward = jnp.where(from_prev, pos < HALF - 1, pos > 0)
-
-            @pl.loop(0, chunks)
-            def _(chunk):
-                @pl.when(onward)
-                def _():
-                    chain(slot, chunk, from_prev, 0).wait_send()
-
-                hand_over(slot, chunk).wait_send()
+            chain_thin(z, chunk, 1).wait_send()
+            hand_full(z, chunk).wait_send()
+
+            @pl.loop(1, 4)
+            def _(far):
+                chain_full(toward_out(far), chunk, 0).wait_send()
+                hand_full(toward_out(far), chunk).wait_send()
+
+            @pl.loop(1, 5)
+            def _(far):
+                chain_thin(toward_out(-far), chunk, 0).wait_send()
+                hand_full(toward_out(-far), chunk).wait_send()
+
+    @pl.when(edge)
+    def _():
+        for i in range(2):
+            ward_weights(i).wait_send()
+
+    @pl.when(inner)
+    def _():
+        @pl.loop(0, RING)
+        def _(slot):
+            pg_copy(slot).wait_send()
+
+        @pl.loop(0, gd_out.shape[0])
+        def _(b):
+            gd_copy(b).wait_send()
 
     out_up.wait()
     out_dn.wait()
@@ -544,6 +684,8 @@
             pltpu.VMEM((model_width, hidden), BF16),
             pltpu.VMEM((hidden, model_width), BF16),
             pltpu.VMEM((model_width, hidden), BF16),
+            pltpu.VMEM((hidden, model_width), BF16),
+            pltpu.VMEM((model_width, hidden), BF16),
             pltpu.VMEM((model_width, hidden), BF16),
             pltpu.VMEM((hidden, model_width), BF16),
             pltpu.VMEM((hidden, model_width), BF16),
@@ -553,11 +695,15 @@
             pltpu.VMEM((PARTS * 2 * UNIT, ALL), BF16),
             pltpu.VMEM((chunks, COLS, MSG, WIDTH), BF16),
             pltpu.VMEM((chunks, COLS, MSG, WIDTH), BF16),
-            pltpu.VMEM((RING, 2, chunks, UNIT, PARTS * WIDTH), BF16),
-            pltpu.VMEM((chunks, UNIT, PARTS * WIDTH), BF16),
-            pltpu.VMEM((chunks, UNIT, PARTS * WIDTH), BF16),
+            pltpu.VMEM((RING, 2, chunks, 2, UNIT, 2 * WIDTH), BF16),
+            pltpu.VMEM((chunks, 2, UNIT, 2 * WIDTH), BF16),
+            pltpu.VMEM((chunks, 2, UNIT, 2 * WIDTH), BF16),
             pltpu.VMEM((hidden, model_width), F32),
-            pltpu.VMEM((hidden, model_width), F32),
+            pltpu.VMEM((2 * hidden, model_width), F32),
+            pltpu.VMEM((RING, 2 * UNIT, hidden), BF16),
+            pltpu.VMEM((RING, 2 * UNIT, hidden), BF16),
+            pltpu.VMEM((7, hidden, model_width // 7), BF16),
+            pltpu.VMEM((7, hidden, model_width // 7), BF16),
             pltpu.VMEM((model_width, hidden), BF16),
             pltpu.VMEM((model_width, hidden), BF16),
             pltpu.VMEM((2 * COLS, tile_rows, hidden), BF16),
@@ -579,6 +725,12 @@
             dma((chunks,)),
             dma((RING, chunks)),
             dma((RING, chunks)),
+            dma((2,)),
+            dma((2,)),
+            dma((RING,)),
+            dma((RING,)),
+            dma((7,)),
+            dma((7,)),
             dma((2, 2)),
             dma((2, 2)),
             dma((2, 2, 2)),
@@ -589,7 +741,7 @@
             dma((2,)),
         ],
         compiler_params=pltpu.CompilerParams(
-            collective_id=0, has_side_effects=True, vmem_limit_bytes=60 * 1024 * 1024
+            collective_id=0, has_side_effects=True, vmem_limit_bytes=62 * 1024 * 1024
         ),
         name="expert_steps",
     )(leaving, adopt, routes, gates, tokens, cotangent, w_up, w_down, m_up, v_up, m_down, v_down)

time: 219 us -> 235 us (1.073)
  Pallas kernels: 212 us -> 228 us
    pallas_call x1, Pallas kernels: 212 us -> 228 us  [expert_steps(): pl.pallas_call(kernel, out_shape=(jax.ShapeDtypeStruct((model_width, hidd...]
where the time goes in v3:
time: 235 us
  Pallas kernels  228 us (97%)
  local copies, waits for them, and re-layouts  5.19 us (2%)
    pallas_call x1, Pallas kernels, expert_steps(): pl.pallas_call(kernel, out_shape=(jax.ShapeDtypeStruct((model_width, hidd...  228 us
    unnamed x12, local copies, waits for them, and re-layouts  5.19 us

profile of v3, /device:TPU:24, one launch (start us, length us, event | category | flops | bytes accessed | tf_op | source)
XLA Modules:
  0.0 234.9 jit_solution(7963597074519881206)
XLA Ops:
  1.3 0.0 copy-start.3
  1.3 0.6 copy-done.3
  1.9 0.6 select_reduce_fusion.adopt_ref
  2.6 227.8 %expert_steps.1 = (bf16[3584,128]{1,0:T(8,128)(2,1)}, bf16[128,3584]{1,0:T(8,128)(2,1)}, bf16[112,128]{1,0:T(8,128)(2,1)}, bf16[112,128]{1,0:T(8,128)(2,1)}) custom-call(s32[1,1]{1,0:T(1,128)} %bitcast.13.leaving_ref, s32[32]{0:T(128)} %select_reduce_fusion.adopt_ref, s32[1,128]{1,0:T(1,128)} %bitcast.24, f32[1,128]{1,0:T(1,128)} %bitcast.25, ...), custom_call_target="tpu_custom_call" | custom-call | tf_op jit(solution)/shard_map/expert_steps/pallas_call | solution.py:671
  230.4 0.0 copy-start
  230.4 2.2 copy.21
  232.6 0.0 copy-done
  232.6 0.0 copy-start.2
  232.6 0.9 copy.22
  233.6 0.0 copy-done.2
  233.6 0.0 copy-start.1
  233.6 0.6 copy.23
  234.2 0.1 copy-done.1
  234.3 0.6 copy.24
Async XLA Ops:
  1.3 0.7 copy-start.3
  230.4 2.3 copy-start
  232.6 0.9 copy-start.2
  233.6 0.8 copy-start.1

commit v4 on v3

--- a/solution.py
+++ b/solution.py
@@ -25,6 +25,7 @@
 MSG = PARTS * 2 * SLOTS
 UNIT = COLS * SLOTS
 ALL = COLS * MSG
+LAG = 3
 
 
 def mul_t(a, b):
@@ -433,21 +434,31 @@
         for i in range(2):
             ward_weights(i).wait_recv()
 
-        @pl.loop(1, HALF)
-        def _(k):
-            @pl.loop(0, chunks)
-            def _(chunk):
-                relay_out(k, chunk)
-                relay_in(k + 1, chunk)
-                first = chunk == 2
-
-                @pl.when(first | (chunk == 5))
-                def _():
-                    terms_inner(toward_out(jnp.where(first, k - 1, -k)))
-
-        @pl.loop(0, 2)
+        def relay_in_at(item):
+            relay_in(item // chunks + 1, lax.rem(item, chunks))
+
+        steps = (HALF - 1) * chunks
+
+        @pl.loop(0, steps)
+        def _(item):
+            relay_out(item // chunks + 1, lax.rem(item, chunks))
+
+            @pl.when(item >= LAG)
+            def _():
+                relay_in_at(item + chunks - LAG)
+
+            @pl.when(lax.rem(item, 3) == 2)
+            def _():
+                turn = item // 3
+                terms_inner(
+                    toward_out(jnp.where(lax.rem(turn, 2) == 0, turn // 2, -((turn + 1) // 2)))
+                )
+
+        @pl.loop(0, LAG)
         def _(i):
-            terms_inner(toward_out(jnp.where(i == 0, HALF - 1, -HALF)))
+            relay_in_at(steps + chunks - LAG + i)
+
+        terms_inner(toward_out(-HALF))
 
         span = gd_out.shape[2]
         for b in range(gd_out.shape[0]):

time: 235 us -> 191 us (0.81)
  Pallas kernels: 228 us -> 184 us
    pallas_call x1, Pallas kernels: 228 us -> 184 us  [expert_steps(): pl.pallas_call(kernel, out_shape=(jax.ShapeDtypeStruct((model_width, hidd...]
where the time goes in v4:
time: 191 us
  Pallas kernels  184 us (96%)
  local copies, waits for them, and re-layouts  5.19 us (3%)
    pallas_call x1, Pallas kernels, expert_steps(): pl.pallas_call(kernel, out_shape=(jax.ShapeDtypeStruct((model_width, hidd...  184 us
    unnamed x12, local copies, waits for them, and re-layouts  5.19 us

profile of v4, /device:TPU:24, one launch (start us, length us, event | category | flops | bytes accessed | tf_op | source)
XLA Modules:
  0.0 190.7 jit_solution(13711428909696245330)
XLA Ops:
  1.3 0.0 copy-start.3
  1.3 0.6 copy-done.3
  1.9 0.6 select_reduce_fusion.adopt_ref
  2.6 183.6 %expert_steps.1 = (bf16[3584,128]{1,0:T(8,128)(2,1)}, bf16[128,3584]{1,0:T(8,128)(2,1)}, bf16[112,128]{1,0:T(8,128)(2,1)}, bf16[112,128]{1,0:T(8,128)(2,1)}) custom-call(s32[1,1]{1,0:T(1,128)} %bitcast.13.leaving_ref, s32[32]{0:T(128)} %select_reduce_fusion.adopt_ref, s32[1,128]{1,0:T(1,128)} %bitcast.24, f32[1,128]{1,0:T(1,128)} %bitcast.25, ...), custom_call_target="tpu_custom_call" | custom-call | tf_op jit(solution)/shard_map/expert_steps/pallas_call | solution.py:682
  186.1 0.0 copy-start
  186.1 2.2 %copy.21 = bf16[1,3584,128]{2,1,0:T(8,128)(2,1)} copy(bf16[1,3584,128]{2,1,0:T(8,128)(2,1)} %bitcast.15) | data formatting | bytes 1835008
  188.4 0.0 copy-done
  188.4 0.0 copy-start.2
  188.4 0.9 copy.22
  189.3 0.0 copy-done.2
  189.3 0.0 copy-start.1
  189.3 0.6 copy.23
  189.9 0.1 copy-done.1
  190.1 0.6 copy.24
Async XLA Ops:
  1.3 0.7 copy-start.3
  186.1 2.3 %copy-start = (bf16[128,3584]{1,0:T(8,128)(2,1)S(1)}, bf16[128,3584]{1,0:T(8,128)(2,1)}, u32[]{:S(2)}) copy-start(bf16[128,3584]{1,0:T(8,128)(2,1)} %get-tuple-element.9) | copy-start | bytes 2752516
  188.4 0.9 copy-start.2
  189.3 0.8 copy-start.1

commit v5 on v4

--- a/solution.py
+++ b/solution.py
@@ -25,7 +25,7 @@
 MSG = PARTS * 2 * SLOTS
 UNIT = COLS * SLOTS
 ALL = COLS * MSG
-LAG = 3
+LAG = 2
 
 
 def mul_t(a, b):
@@ -43,11 +43,11 @@
 
 
 def kernel(
-    leaving_ref, adopt_ref, routes_ref, gates_ref, tok_hbm, cot_hbm, wup_hbm, wdn_hbm, mup_hbm, vup_hbm, mdn_hbm, vdn_hbm,
-    sup_hbm, sdn_hbm, aup_ref, adn_ref,
+    leaving_ref, owner_ref, routes_ref, gates_ref, tok_hbm, cot_hbm, wup_hbm, wdn_hbm, mup_hbm, vup_hbm, mdn_hbm, vdn_hbm,
+    sup_hbm, sdn_hbm, adopted_ref,
     tok, cot, wup, wdn, wup_ward, wdn_ward, mup, vup, mdn, vdn, sup, sdn,
     pick, unpick, packed, landed, own, other, transit, gup, gdn, pg_out, pg_in, gd_out, gd_in,
-    leave_up, leave_dn, by_tile, tiles, hop, got, summed, fin, last,
+    adopt_ref, leave_up, leave_dn, by_tile, tiles, hop, got, summed, fin, last,
     load_sem, out_sem, plane_send, plane_recv, plane_self,
     chain_send, chain_recv, other_send, transit_send, transit_recv, mate_send, mate_recv,
     ward_send, ward_recv, pg_send, pg_recv, gd_send, gd_recv, hop_send, hop_recv, ring_send, ring_recv, fin_send, fin_recv, last_send, last_recv,
@@ -132,7 +132,7 @@
     z_in = lax.rem(z + RING - out_sign, RING)
 
     def ward_weights(i):
-        src, dst = ((wup_hbm, wup_ward), (wdn_hbm, wdn_ward))[i]
+        src, dst = ((wup, wup_ward), (wdn, wdn_ward))[i]
         return pltpu.make_async_remote_copy(
             src_ref=src,
             dst_ref=dst,
@@ -142,13 +142,14 @@
             device_id_type=MESH,
         )
 
+    for load in loads[:4]:
+        load.wait()
+
     @pl.when(edge)
     def _():
         for i in range(2):
             ward_weights(i).start()
 
-    loads[0].wait()
-    loads[1].wait()
 
     def lanes(chunk, high):
         return pl.ds(pl.multiple_of(high * half_width + chunk * WIDTH, 128), WIDTH)
@@ -182,6 +183,13 @@
         @pl.loop(1, COLS)
         def _(i):
             plane_copy(chunk, i).start()
+
+    @pl.loop(0, 2 * COLS)
+    def _(owner):
+        mine = jnp.int32(0)
+        for tile in range(2 * COLS):
+            mine = jnp.where(owner_ref[tile] == owner, jnp.int32(tile), mine)
+        adopt_ref[owner] = mine
 
     line = lax.broadcasted_iota(jnp.int32, (UNIT, ALL), 0)
     source = lax.broadcasted_iota(jnp.int32, (UNIT, ALL), 1)
@@ -318,7 +326,7 @@
             chain_thin(z, chunk, 1).start()
             hand_full(z, chunk).start()
 
-    for load in loads[2:]:
+    for load in loads[4:]:
         load.wait()
 
     hidden_units = wup.shape[1]
@@ -547,7 +555,7 @@
     def _(b):
         at = pl.ds(pl.multiple_of(b * block, block), block)
         step = adam_step(gup[:, at].T, mup[at, :], vup[at, :])
-        sup[at, :] = jnp.where(leaves, 0.0, step).astype(BF16)
+        sup[at, :] = step.astype(BF16)
         leave_up[at, :] = jnp.where(leaves, step, 0.0).astype(BF16)
 
     out_up = pltpu.make_async_copy(sup, sup_hbm, out_sem.at[0])
@@ -576,7 +584,7 @@
         def _(i):
             at = pl.ds(pl.multiple_of(b * span + i * block, block), block)
             step = adam_step(gdn[0:hidden_units, at], mdn[:, at], vdn[:, at])
-            sdn[:, at] = jnp.where(leaves, 0.0, step).astype(BF16)
+            sdn[:, at] = step.astype(BF16)
             leave_dn[at, :] = jnp.where(leaves, step, 0.0).T.astype(BF16)
 
     out_dn = pltpu.make_async_copy(sdn, sdn_hbm, out_sem.at[1])
@@ -600,9 +608,9 @@
         summed[axis, mine] = summed[axis, mine] + fin[axis, 0] + fin[axis, 1] + fin[axis, 2]
         last_copy(axis).start()
 
-    for axis, adopted in ((0, aup_ref), (1, adn_ref)):
+    for axis in range(2):
         last_copy(axis).wait_recv()
-        adopted[...] = summed[axis, line_at[axis] * 2 + zhi] + last[axis]
+        adopted_ref[axis] = summed[axis, line_at[axis] * 2 + zhi] + last[axis]
 
     for axis in range(2):
         for side in range(2):
@@ -670,11 +678,11 @@
     out_dn.wait()
 
 
-def expert_steps(leaving, adopt, routes, gates, tokens, cotangent, w_up, w_down, m_up, v_up, m_down, v_down):
+def expert_steps(leaving, tile_owner, routes, gates, tokens, cotangent, w_up, w_down, m_up, v_up, m_down, v_down):
     count, model_width = tokens.shape
     hidden = w_up.shape[1]
     chunks = model_width // 2 // WIDTH
-    tile_rows = model_width // adopt.shape[0]
+    tile_rows = model_width // tile_owner.shape[0]
     smem = pl.BlockSpec(memory_space=pltpu.SMEM)
     vmem = pl.BlockSpec(memory_space=pltpu.VMEM)
     anyw = pl.BlockSpec(memory_space=pl.ANY)
@@ -684,11 +692,10 @@
         out_shape=(
             jax.ShapeDtypeStruct((model_width, hidden), BF16),
             jax.ShapeDtypeStruct((hidden, model_width), BF16),
-            jax.ShapeDtypeStruct((tile_rows, hidden), BF16),
-            jax.ShapeDtypeStruct((tile_rows, hidden), BF16),
+            jax.ShapeDtypeStruct((2, tile_rows, hidden), BF16),
         ),
         in_specs=[vmem, smem, vmem, vmem] + [anyw] * 8,
-        out_specs=(anyw, anyw, vmem, vmem),
+        out_specs=(anyw, anyw, vmem),
         scratch_shapes=[
             pltpu.VMEM((count, model_width), BF16),
             pltpu.VMEM((count, model_width), BF16),
@@ -715,6 +722,7 @@
             pltpu.VMEM((RING, 2 * UNIT, hidden), BF16),
             pltpu.VMEM((7, hidden, model_width // 7), BF16),
             pltpu.VMEM((7, hidden, model_width // 7), BF16),
+            pltpu.SMEM((2 * COLS,), jnp.int32),
             pltpu.VMEM((model_width, hidden), BF16),
             pltpu.VMEM((model_width, hidden), BF16),
             pltpu.VMEM((2 * COLS, tile_rows, hidden), BF16),
@@ -752,24 +760,19 @@
             dma((2,)),
         ],
         compiler_params=pltpu.CompilerParams(
-            collective_id=0, has_side_effects=True, vmem_limit_bytes=62 * 1024 * 1024
+            collective_id=0, has_side_effects=True, vmem_limit_bytes=52 * 1024 * 1024
         ),
         name="expert_steps",
-    )(leaving, adopt, routes, gates, tokens, cotangent, w_up, w_down, m_up, v_up, m_down, v_down)
+    )(leaving, tile_owner, routes, gates, tokens, cotangent, w_up, w_down, m_up, v_up, m_down, v_down)
 
 
 def on_device(
     tokens, cotangent, gates, routes, w_up, w_down, m_up, v_up, m_down, v_down, leaving, tile_owner
 ):
-    experts = lax.axis_size("expert")
     tok_count = tokens.shape[0]
-    slot_ids = jnp.arange(experts, dtype=jnp.int32)
-    adopt = jnp.sum(
-        jnp.where(tile_owner[None, :] == slot_ids[:, None], slot_ids[None, :], 0), axis=1
-    )
-    outs = expert_steps(
+    step_up, step_down, adopted = expert_steps(
         leaving.reshape(1, 1),
-        adopt,
+        tile_owner,
         routes.reshape(1, tok_count),
         gates.reshape(1, tok_count),
         tokens,
@@ -781,7 +784,10 @@
         m_down[0],
         v_down[0],
     )
-    return tuple(out[None] for out in outs)
+    keep_own = lax.axis_index("expert") != leaving[0]
+    update_up = jnp.where(keep_own, step_up, jnp.zeros_like(step_up))[None]
+    update_down = jnp.where(keep_own, step_down, jnp.zeros_like(step_down))[None]
+    return (update_up, update_down, adopted[0][None], adopted[1][None])
 
 
 def solution(mesh):

time: 191 us -> 187 us (0.979)
  local copies, waits for them, and re-layouts: 5.19 us -> 1.28 us
  Pallas kernels: 184 us -> 182 us
    unnamed x12 -> x6, local copies, waits for them, and re-layouts: 5.19 us -> 0.66 us
    broadcast_in_dim x0 -> x2, other arithmetic: none -> 1.97 us  [the longest x1 0.99 us: on_device(): update_up = jnp.where(keep_own, step_up, jnp.zeros_like(step_up))[None]]
where the time goes in v5:
time: 187 us
  Pallas kernels  182 us (97%)
  other arithmetic  1.97 us (1%)
    pallas_call x1, Pallas kernels, expert_steps(): pl.pallas_call(kernel, out_shape=(jax.ShapeDtypeStruct((model_width, hidd...  182 us

profile of v5, /device:TPU:24, one launch (start us, length us, event | category | flops | bytes accessed | tf_op | source)
XLA Modules:
  0.0 187.0 jit_solution(5691059635031190178)
XLA Ops:
  1.3 0.0 copy-start
  1.3 0.0 copy-start.1
  1.3 0.0 copy-start.2
  1.3 0.6 copy-done
  1.9 0.0 copy-done.1
  2.0 0.0 copy-done.2
  2.0 182.4 %expert_steps.1 = (bf16[3584,128]{1,0:T(8,128)(2,1)S(1)}, bf16[128,3584]{1,0:T(8,128)(2,1)S(1)}, bf16[2,112,128]{2,1,0:T(8,128)(2,1)S(1)}) custom-call(s32[1,1]{1,0:T(1,128)} %bitcast.15.leaving_ref, s32[32]{0:T(128)S(1)} %copy-done, s32[1,128]{1,0:T(1,128)S(1)} %bitcast.16, f32[1,128]{1,0:T(1,128)S(1)} %bitcast.17, bf16[128,3584]{1,0:T(8,128)(2,1)} %tok_hbm.1, ...), custom_call_target="tpu_custom_call" | custom-call | tf_op jit(solution)/shard_map/expert_steps/pallas_call | solution.py:690
  184.4 1.0 select_bitcast_fusion.1
  185.4 1.0 select_bitcast_fusion
  186.4 0.6 fusion
Async XLA Ops:
  1.3 0.7 copy-start
  1.3 0.7 copy-start.1
  1.3 0.7 copy-start.2

commit v6 on v5

--- a/solution.py
+++ b/solution.py
@@ -44,11 +44,11 @@
 
 def kernel(
     leaving_ref, owner_ref, routes_ref, gates_ref, tok_hbm, cot_hbm, wup_hbm, wdn_hbm, mup_hbm, vup_hbm, mdn_hbm, vdn_hbm,
-    sup_hbm, sdn_hbm, adopted_ref,
-    tok, cot, wup, wdn, wup_ward, wdn_ward, mup, vup, mdn, vdn, sup, sdn,
+    sup, sdn, adopted_ref,
+    tok, cot, wup, wdn, wup_ward, wdn_ward, mup, vup, mdn, vdn,
     pick, unpick, packed, landed, own, other, transit, gup, gdn, pg_out, pg_in, gd_out, gd_in,
     adopt_ref, leave_up, leave_dn, by_tile, tiles, hop, got, summed, fin, last,
-    load_sem, out_sem, plane_send, plane_recv, plane_self,
+    load_sem, plane_send, plane_recv, plane_self,
     chain_send, chain_recv, other_send, transit_send, transit_recv, mate_send, mate_recv,
     ward_send, ward_recv, pg_send, pg_recv, gd_send, gd_recv, hop_send, hop_recv, ring_send, ring_recv, fin_send, fin_recv, last_send, last_recv,
 ):
@@ -558,8 +558,6 @@
         sup[at, :] = step.astype(BF16)
         leave_up[at, :] = jnp.where(leaves, step, 0.0).astype(BF16)
 
-    out_up = pltpu.make_async_copy(sup, sup_hbm, out_sem.at[0])
-    out_up.start()
     sort_tiles(0, leave_up)
 
     def pass_on(axis):
@@ -570,7 +568,6 @@
             tiles[axis, to, part] = tiles[axis, to, part] + hop[axis, side]
             ring_copy(axis, side, 1).start()
 
-    pass_on(0)
     span = gd_in.shape[2]
 
     @pl.loop(0, gd_in.shape[0])
@@ -587,8 +584,7 @@
             sdn[:, at] = step.astype(BF16)
             leave_dn[at, :] = jnp.where(leaves, step, 0.0).T.astype(BF16)
 
-    out_dn = pltpu.make_async_copy(sdn, sdn_hbm, out_sem.at[1])
-    out_dn.start()
+    pass_on(0)
     sort_tiles(1, leave_dn)
 
     pass_on(1)
@@ -673,9 +669,6 @@
         @pl.loop(0, gd_out.shape[0])
         def _(b):
             gd_copy(b).wait_send()
-
-    out_up.wait()
-    out_dn.wait()
 
 
 def expert_steps(leaving, tile_owner, routes, gates, tokens, cotangent, w_up, w_down, m_up, v_up, m_down, v_down):
@@ -695,7 +688,7 @@
             jax.ShapeDtypeStruct((2, tile_rows, hidden), BF16),
         ),
         in_specs=[vmem, smem, vmem, vmem] + [anyw] * 8,
-        out_specs=(anyw, anyw, vmem),
+        out_specs=(vmem, vmem, vmem),
         scratch_shapes=[
             pltpu.VMEM((count, model_width), BF16),
             pltpu.VMEM((count, model_width), BF16),
@@ -706,8 +699,6 @@
             pltpu.VMEM((model_width, hidden), BF16),
             pltpu.VMEM((model_width, hidden), BF16),
             pltpu.VMEM((hidden, model_width), BF16),
-            pltpu.VMEM((hidden, model_width), BF16),
-            pltpu.VMEM((model_width, hidden), BF16),
             pltpu.VMEM((hidden, model_width), BF16),
             pltpu.VMEM((ALL, PARTS * count), BF16),
             pltpu.VMEM((PARTS * 2 * UNIT, ALL), BF16),
@@ -733,7 +724,6 @@
             pltpu.VMEM((2, SIDE - 1, 2, tile_rows, hidden), BF16),
             pltpu.VMEM((2, tile_rows, hidden), BF16),
             dma((8,)),
-            dma((2,)),
             dma((chunks, COLS)),
             dma((chunks, COLS)),
             dma((chunks,)),

time: 187 us -> 187 us (level)
  no operation moved by 1% of the time
where the time goes in v6:
time: 187 us
  Pallas kernels  182 us (97%)
  other arithmetic  1.97 us (1%)
    pallas_call x1, Pallas kernels, expert_steps(): pl.pallas_call(kernel, out_shape=(jax.ShapeDtypeStruct((model_width, hidd...  182 us

profile of v6, /device:TPU:24, one launch (start us, length us, event | category | flops | bytes accessed | tf_op | source)
XLA Modules:
  0.0 186.8 jit_solution(7521009818874532937)
XLA Ops:
  1.3 0.0 copy-start
  1.3 0.0 copy-start.1
  1.3 0.0 copy-start.2
  1.3 0.6 copy-done
  1.9 0.0 copy-done.1
  2.0 0.0 copy-done.2
  2.0 182.2 %expert_steps.1 = (bf16[3584,128]{1,0:T(8,128)(2,1)S(1)}, bf16[128,3584]{1,0:T(8,128)(2,1)S(1)}, bf16[2,112,128]{2,1,0:T(8,128)(2,1)S(1)}) custom-call(s32[1,1]{1,0:T(1,128)} %bitcast.15.leaving_ref, s32[32]{0:T(128)S(1)} %copy-done, s32[1,128]{1,0:T(1,128)S(1)} %bitcast.16, f32[1,128]{1,0:T(1,128)S(1)} %bitcast.17, bf16[128,3584]{1,0:T(8,128)(2,1)} %tok_hbm.1, ...), custom_call_target="tpu_custom_call" | custom-call | tf_op jit(solution)/shard_map/expert_steps/pallas_call | solution.py:683
  184.2 1.0 select_bitcast_fusion.1
  185.2 1.0 select_bitcast_fusion
  186.2 0.6 fusion
Async XLA Ops:
  1.3 0.7 copy-start
  1.3 0.7 copy-start.1
  1.3 0.7 copy-start.2
